TPU v7x, 512 devices: a whole 4x4x16 slice. The times are simulated.
512 devices in a mesh: section: 16 (over z), dp: 32 (over y, x, core).
Axes of the slice: x: 4, y: 4, z: 16, core: 2. Of those that a mesh axis runs over, the one named last changes fastest.
Arguments:
- acts: bfloat16 [16, 4, 32, 12, 16, 512], P('section', None, 'dp'), may hold values from -6 to 6
- out_grad: bfloat16 [4, 32, 12, 16, 512], P(None, 'dp'), may hold values from -6 to 6
- depth_kernel: bfloat16 [16, 3, 3, 512], P('section'), may hold values from -2 to 2
- point_weight: bfloat16 [16, 512, 512], P('section'), may hold values from -0.25 to 0.25
- bn_gain: float32 [16, 512], P('section'), may hold values from 0.15 to 0.45
Outputs:
- act_grad: bfloat16 [16, 4, 32, 12, 16, 512], P('section', None, 'dp')
- point_grad: float32 [16, 512, 512], P('section')
- kernel_grad: float32 [16, 3, 3, 512], P('section')
- gain_grad: float32 [16, 512], P('section')
- bias_grad: float32 [16, 512], P('section')
All inputs are finite; a program needn't handle non-finite values.
Results may differ from a plain program's by a relative error of at most 0.025.
Values may be sent and summed in bfloat16 or wider, within the bound.
A program may use at most 64 MiB of HBM per device.

v0:
```python
import jax
import jax.numpy as jnp
from jax import lax
from jax.sharding import PartitionSpec as P

epsilon = 1e-05


def from_everyone(x, axis):
    copies = jnp.broadcast_to(x, (lax.axis_size(axis), *x.shape))
    return lax.all_to_all(copies, axis, split_axis=0, concat_axis=0, tiled=True)


def taken_together(x, axis):
    everything = from_everyone(x, axis)
    return jnp.sum(everything, axis=0)


def in_one(arrays, axis):
    ravelled, at, finished = (jnp.concatenate([a.reshape(-1) for a in arrays]), 0, [])
    running = taken_together(ravelled, axis)
    for a in arrays:
        finished.append(running[at : at + a.size].reshape(a.shape))
        at += a.size
    return tuple(finished)


def shifted(x, axis, by):
    length = lax.axis_size(axis)
    pairs = [(i, i + by) for i in range(length) if 0 <= i + by < length]
    return lax.ppermute(x, axis, pairs)


def depthwise(active, kernel):
    padded = jnp.pad(active, ((0, 0), (1, 1), (1, 1), (0, 0)))
    height, width = (active.shape[1], active.shape[2])
    summed = jnp.zeros(active.shape, jnp.float32)
    for row_off in range(3):
        for col_off in range(3):
            summed = (
                summed
                + kernel[row_off, col_off]
                * padded[:, row_off : row_off + height, col_off : col_off + width]
            )
    return summed


def depthwise_back(grad, kernel):
    padded = jnp.pad(grad, ((0, 0), (1, 1), (1, 1), (0, 0)))
    height, width = (grad.shape[1], grad.shape[2])
    summed = jnp.zeros(grad.shape, jnp.float32)
    for row_off in range(3):
        for col_off in range(3):
            summed = (
                summed
                + kernel[row_off, col_off]
                * padded[:, 2 - row_off : 2 - row_off + height, 2 - col_off : 2 - col_off + width]
            )
    return summed


def kernel_terms(active, grad):
    padded = jnp.pad(active, ((0, 0), (1, 1), (1, 1), (0, 0)))
    height, width = (active.shape[1], active.shape[2])
    table = []
    for row_off in range(3):
        line = []
        for col_off in range(3):
            line.append(
                jnp.sum(
                    padded[:, row_off : row_off + height, col_off : col_off + width] * grad,
                    axis=(0, 1, 2),
                )
            )
        table.append(jnp.stack(line))
    return jnp.stack(table)


def pick(array, slot):
    return lax.dynamic_index_in_dim(array, slot, 0, keepdims=False)


def body(acts, out_grad, depth_kernel, point_weight, bn_gain):
    sections = lax.axis_size("section")
    replicas = lax.axis_size("dp")
    my_section = lax.axis_index("section")
    micros, images, height, width, channels = acts.shape[1:]
    rows = images * height * width
    count = images * replicas * height * width
    shape = (images, height, width, channels)
    inputs = acts[0]
    kernel = depth_kernel[0].astype(jnp.float32)
    weight = point_weight[0]
    gain = bn_gain[0]
    active = jnp.maximum(inputs.astype(jnp.float32), 0.0)
    depth_out = depthwise(active.reshape(micros * images, height, width, channels), kernel).astype(
        jnp.bfloat16
    )
    depth_flat = depth_out.reshape(micros * rows, channels)
    pre_norm = jnp.dot(depth_flat, weight, preferred_element_type=jnp.float32).reshape(
        micros, rows, channels
    )
    pre_bank = jnp.zeros((1,), jnp.bfloat16)
    depth_bank = jnp.zeros((1,), jnp.float32)
    depth_rows = depth_flat.reshape(micros, rows, channels)

    def step(turn, carry):
        incoming, grads_out, gain_acc, bias_acc, point_acc, kernel_acc, pre_store, depth_store = (
            carry
        )
        micro = turn - (sections - 1 - my_section)
        valid = jnp.logical_and(micro >= 0, micro < micros)
        slot = jnp.clip(micro, 0, micros - 1)
        flag = valid.astype(jnp.float32)
        upstream = jnp.where(my_section == sections - 1, pick(out_grad, slot), incoming)
        upstream = upstream.astype(jnp.float32).reshape(rows, channels)
        pre_slot = pick(pre_norm, slot)
        first, second, sum_grad, raw_cross = in_one(
            (
                jnp.sum(pre_slot, axis=0),
                jnp.sum(pre_slot * pre_slot, axis=0),
                jnp.sum(upstream, axis=0),
                jnp.sum(upstream * pre_slot, axis=0),
            ),
            "dp",
        )
        center = first / count
        inv_std = lax.rsqrt(second / count - center * center + epsilon)
        normed = (pre_slot - center) * inv_std
        sum_cross = inv_std * (raw_cross - center * sum_grad)
        pre_grad = (
            gain * inv_std * (upstream - sum_grad / count - normed * sum_cross / count)
        ).astype(jnp.bfloat16)
        depth_grad = lax.dot_general(
            pre_grad, weight, (((1,), (1,)), ((), ())), preferred_element_type=jnp.float32
        ).reshape(shape)
        active_slot = pick(active, slot)
        input_slot = pick(inputs, slot)
        back = depthwise_back(depth_grad, kernel)
        input_grad = (upstream.reshape(shape) + jnp.where(input_slot > 0, back, 0.0)).astype(
            jnp.bfloat16
        )
        gain_acc = gain_acc + flag * sum_cross
        bias_acc = bias_acc + flag * sum_grad
        depth_slot = pick(depth_rows, slot)
        point_acc = point_acc + flag * lax.dot_general(
            depth_slot, pre_grad, (((0,), (0,)), ((), ())), preferred_element_type=jnp.float32
        )
        kernel_acc = kernel_acc + flag * kernel_terms(active_slot, depth_grad)
        kept_grad = jnp.where(valid, input_grad, pick(grads_out, slot))
        grads_out = lax.dynamic_update_index_in_dim(grads_out, kept_grad, slot, 0)
        incoming = shifted(input_grad, "section", -1)
        return (
            incoming,
            grads_out,
            gain_acc,
            bias_acc,
            point_acc,
            kernel_acc,
            pre_store,
            depth_store,
        )

    start = (
        jnp.zeros(shape, jnp.bfloat16),
        jnp.zeros((micros,) + shape, jnp.bfloat16),
        jnp.zeros((channels,), jnp.float32),
        jnp.zeros((channels,), jnp.float32),
        jnp.zeros((channels, channels), jnp.float32),
        jnp.zeros((3, 3, channels), jnp.float32),
        pre_bank,
        depth_bank,
    )
    final = lax.fori_loop(0, sections + micros - 1, step, start)
    grads_out, gain_acc, bias_acc, point_acc, kernel_acc, pre_store, depth_store = final[1:]
    point_sum, kernel_sum = (
        lax.psum(point_acc.astype(jnp.bfloat16), "dp").astype(jnp.float32),
        lax.psum(kernel_acc.astype(jnp.bfloat16), "dp").astype(jnp.float32),
    )
    return (grads_out[None], point_sum[None], kernel_sum[None], gain_acc[None], bias_acc[None])


def solution(mesh):
    return jax.shard_map(
        body,
        mesh=mesh,
        in_specs=(
            P("section", None, "dp", None, None, None),
            P(None, "dp", None, None, None),
            P("section", None, None, None),
            P("section", None, None),
            P("section", None),
        ),
        out_specs=(
            P("section", None, "dp", None, None, None),
            P("section", None, None),
            P("section", None, None, None),
            P("section", None),
            P("section", None),
        ),
        check_vma=False,
    )
```

profile of v0, /device:TPU:1, one launch (start us, length us, event | category | flops | bytes accessed | tf_op | source)
XLA Modules:
  0.0 723.6 jit_solution(13232851758177793527)
XLA Ops:
  20.9 555.3 %while.26 = (s32[]{:T(128)}, bf16[1,12,16,512]{3,2,1,0:T(8,128)(2,1)S(1)}, bf16[4,1,12,16,512]{4,3,2,1,0:T(8,128)(2,1)}, f32[512]{0:T(512)S(1)}, f32[512]{0:T(51...) while((s32[]{:T(128)}, ...), condition=%wide.region_15.16_spmd.clone, body=%wide.region_0.15_spmd.clone.sunk | while | flops 208999424 | bytes 16183717 | solution.py:174
  23.9 10.4 %all-to-all-start = ((f32[32,1,2048]{2,1,0:T(1,128)}), f32[32,1,2048]{2,1,0:T(1,128)S(1)}, u32[]{:S(2)}, u32[]{:S(2)}) async-start(f32[32,1,2048]{2,1,0:T(1,128)} %broadcast_in_dim.88), calls=%async_computation | async-start | bytes 524288 | tf_op jit(solution)/shard_map/while/body/eval_jaxpr/all_to_all | solution.py:11
  36.3 7.0 all-to-all-done
  92.2 7.0 all-to-all-done
  120.1 7.0 all-to-all-done
  148.1 7.0 all-to-all-done
  161.0 7.0 collective-permute-done
  177.3 7.0 all-to-all-done
  190.2 7.0 collective-permute-done
  219.3 7.0 collective-permute-done
  248.5 7.0 collective-permute-done
  277.6 7.0 collective-permute-done
  306.8 7.0 collective-permute-done
  336.0 7.0 collective-permute-done
  365.1 7.0 collective-permute-done
  394.3 7.0 collective-permute-done
  423.4 7.0 collective-permute-done
  452.6 7.0 collective-permute-done
  481.7 7.0 collective-permute-done
  510.9 7.0 collective-permute-done
  540.0 7.0 collective-permute-done
  569.2 7.0 collective-permute-done
  577.1 120.4 %psum.15 = bf16[1,3,3,512]{3,0,2,1:T(2,128)(2,1)S(1)} all-reduce(bf16[1,3,3,512]{3,0,2,1:T(2,128)(2,1)S(1)} %broadcast_in_dim.78), channel_id=1, replica_groups=mesh['section'=16,'dp'=32] {'dp'}, use_global_device_ids=true, to_apply=%region_17.18 | all-reduce | flops 4608 | bytes 18432 | tf_op jit(solution)/shard_map/psum | solution.py:178
  698.1 16.5 %all-reduce.5.cloned.1.call-done = bf16[1,512,512]{2,1,0:T(8,128)(2,1)} async-done(((bf16[1,512,512]{2,1,0:T(8,128)(2,1)}), bf16[1,512,512]{2,1,0:T(8,128)(2,1)}) %all-reduce.5.cloned.1.call-update) | async-done | bytes 524304 | tf_op jit(solution)/shard_map/psum | solution.py:177
  (506 shorter events, 420.7 us)
Async XLA Ops:
  7.2 707.4 %all-reduce.5.cloned.1.call-start = ((), (), s32[]{:S(2)}) async-start(), calls=%async_computation.1 | async-start | bytes 1048576 | tf_op jit(solution)/shard_map/psum | solution.py:177
  23.9 19.4 %all-to-all-start = ((f32[32,1,2048]{2,1,0:T(1,128)}), f32[32,1,2048]{2,1,0:T(1,128)S(1)}, u32[]{:S(2)}, u32[]{:S(2)}) async-start(f32[32,1,2048]{2,1,0:T(1,128)} %broadcast_in_dim.88), calls=%async_computation | async-start | bytes 524288 | tf_op jit(solution)/shard_map/while/body/eval_jaxpr/all_to_all | solution.py:11
  57.7 13.5 %all-to-all-start = ((f32[32,1,2048]{2,1,0:T(1,128)}), f32[32,1,2048]{2,1,0:T(1,128)S(1)}, u32[]{:S(2)}, u32[]{:S(2)}) async-start(f32[32,1,2048]{2,1,0:T(1,128)} %broadcast_in_dim.88), calls=%async_computation | async-start | bytes 524288 | tf_op jit(solution)/shard_map/while/body/eval_jaxpr/all_to_all | solution.py:11
  85.6 13.5 %all-to-all-start = ((f32[32,1,2048]{2,1,0:T(1,128)}), f32[32,1,2048]{2,1,0:T(1,128)S(1)}, u32[]{:S(2)}, u32[]{:S(2)}) async-start(f32[32,1,2048]{2,1,0:T(1,128)} %broadcast_in_dim.88), calls=%async_computation | async-start | bytes 524288 | tf_op jit(solution)/shard_map/while/body/eval_jaxpr/all_to_all | solution.py:11
  113.6 13.5 %all-to-all-start = ((f32[32,1,2048]{2,1,0:T(1,128)}), f32[32,1,2048]{2,1,0:T(1,128)S(1)}, u32[]{:S(2)}, u32[]{:S(2)}) async-start(f32[32,1,2048]{2,1,0:T(1,128)} %broadcast_in_dim.88), calls=%async_computation | async-start | bytes 524288 | tf_op jit(solution)/shard_map/while/body/eval_jaxpr/all_to_all | solution.py:11
  141.6 13.5 %all-to-all-start = ((f32[32,1,2048]{2,1,0:T(1,128)}), f32[32,1,2048]{2,1,0:T(1,128)S(1)}, u32[]{:S(2)}, u32[]{:S(2)}) async-start(f32[32,1,2048]{2,1,0:T(1,128)} %broadcast_in_dim.88), calls=%async_computation | async-start | bytes 524288 | tf_op jit(solution)/shard_map/while/body/eval_jaxpr/all_to_all | solution.py:11
  158.2 9.8 %collective-permute-start = (bf16[1,12,16,512]{3,2,1,0:T(8,128)(2,1)S(1)}, bf16[1,12,16,512]{3,2,1,0:T(8,128)(2,1)S(1)}, u32[]{:S(2)}, u32[]{:S(2)}) collective-permute-start(bf16[1,12,16,512]{3,2,1,0:T(8,128)(2,1)S(1)} %get-tuple-element.682), channel_id=1, source_target_pairs={{32,0},{64,32},{96,64},{128,96},{160,128},{192,160},{224,192},{256... | collective-permute-start | bytes 589832 | tf_op jit(solution)/shard_map/while/body/eval_jaxpr/ppermute | solution.py:31
  171.0 13.2 %all-to-all-start = ((f32[32,1,2048]{2,1,0:T(1,128)}), f32[32,1,2048]{2,1,0:T(1,128)S(1)}, u32[]{:S(2)}, u32[]{:S(2)}) async-start(f32[32,1,2048]{2,1,0:T(1,128)} %broadcast_in_dim.88), calls=%async_computation | async-start | bytes 524288 | tf_op jit(solution)/shard_map/while/body/eval_jaxpr/all_to_all | solution.py:11
  200.2 13.2 %all-to-all-start = ((f32[32,1,2048]{2,1,0:T(1,128)}), f32[32,1,2048]{2,1,0:T(1,128)S(1)}, u32[]{:S(2)}, u32[]{:S(2)}) async-start(f32[32,1,2048]{2,1,0:T(1,128)} %broadcast_in_dim.88), calls=%async_computation | async-start | bytes 524288 | tf_op jit(solution)/shard_map/while/body/eval_jaxpr/all_to_all | solution.py:11
  216.5 9.8 %collective-permute-start = (bf16[1,12,16,512]{3,2,1,0:T(8,128)(2,1)S(1)}, bf16[1,12,16,512]{3,2,1,0:T(8,128)(2,1)S(1)}, u32[]{:S(2)}, u32[]{:S(2)}) collective-permute-start(bf16[1,12,16,512]{3,2,1,0:T(8,128)(2,1)S(1)} %get-tuple-element.682), channel_id=1, source_target_pairs={{32,0},{64,32},{96,64},{128,96},{160,128},{192,160},{224,192},{256... | collective-permute-start | bytes 589832 | tf_op jit(solution)/shard_map/while/body/eval_jaxpr/ppermute | solution.py:31
  229.3 13.2 %all-to-all-start = ((f32[32,1,2048]{2,1,0:T(1,128)}), f32[32,1,2048]{2,1,0:T(1,128)S(1)}, u32[]{:S(2)}, u32[]{:S(2)}) async-start(f32[32,1,2048]{2,1,0:T(1,128)} %broadcast_in_dim.88), calls=%async_computation | async-start | bytes 524288 | tf_op jit(solution)/shard_map/while/body/eval_jaxpr/all_to_all | solution.py:11
  245.6 9.8 %collective-permute-start = (bf16[1,12,16,512]{3,2,1,0:T(8,128)(2,1)S(1)}, bf16[1,12,16,512]{3,2,1,0:T(8,128)(2,1)S(1)}, u32[]{:S(2)}, u32[]{:S(2)}) collective-permute-start(bf16[1,12,16,512]{3,2,1,0:T(8,128)(2,1)S(1)} %get-tuple-element.682), channel_id=1, source_target_pairs={{32,0},{64,32},{96,64},{128,96},{160,128},{192,160},{224,192},{256... | collective-permute-start | bytes 589832 | tf_op jit(solution)/shard_map/while/body/eval_jaxpr/ppermute | solution.py:31
  258.5 13.2 %all-to-all-start = ((f32[32,1,2048]{2,1,0:T(1,128)}), f32[32,1,2048]{2,1,0:T(1,128)S(1)}, u32[]{:S(2)}, u32[]{:S(2)}) async-start(f32[32,1,2048]{2,1,0:T(1,128)} %broadcast_in_dim.88), calls=%async_computation | async-start | bytes 524288 | tf_op jit(solution)/shard_map/while/body/eval_jaxpr/all_to_all | solution.py:11
  274.8 9.8 %collective-permute-start = (bf16[1,12,16,512]{3,2,1,0:T(8,128)(2,1)S(1)}, bf16[1,12,16,512]{3,2,1,0:T(8,128)(2,1)S(1)}, u32[]{:S(2)}, u32[]{:S(2)}) collective-permute-start(bf16[1,12,16,512]{3,2,1,0:T(8,128)(2,1)S(1)} %get-tuple-element.682), channel_id=1, source_target_pairs={{32,0},{64,32},{96,64},{128,96},{160,128},{192,160},{224,192},{256... | collective-permute-start | bytes 589832 | tf_op jit(solution)/shard_map/while/body/eval_jaxpr/ppermute | solution.py:31
  287.6 13.2 %all-to-all-start = ((f32[32,1,2048]{2,1,0:T(1,128)}), f32[32,1,2048]{2,1,0:T(1,128)S(1)}, u32[]{:S(2)}, u32[]{:S(2)}) async-start(f32[32,1,2048]{2,1,0:T(1,128)} %broadcast_in_dim.88), calls=%async_computation | async-start | bytes 524288 | tf_op jit(solution)/shard_map/while/body/eval_jaxpr/all_to_all | solution.py:11
  316.8 13.2 %all-to-all-start = ((f32[32,1,2048]{2,1,0:T(1,128)}), f32[32,1,2048]{2,1,0:T(1,128)S(1)}, u32[]{:S(2)}, u32[]{:S(2)}) async-start(f32[32,1,2048]{2,1,0:T(1,128)} %broadcast_in_dim.88), calls=%async_computation | async-start | bytes 524288 | tf_op jit(solution)/shard_map/while/body/eval_jaxpr/all_to_all | solution.py:11
  345.9 13.2 %all-to-all-start = ((f32[32,1,2048]{2,1,0:T(1,128)}), f32[32,1,2048]{2,1,0:T(1,128)S(1)}, u32[]{:S(2)}, u32[]{:S(2)}) async-start(f32[32,1,2048]{2,1,0:T(1,128)} %broadcast_in_dim.88), calls=%async_computation | async-start | bytes 524288 | tf_op jit(solution)/shard_map/while/body/eval_jaxpr/all_to_all | solution.py:11
  375.1 13.2 %all-to-all-start = ((f32[32,1,2048]{2,1,0:T(1,128)}), f32[32,1,2048]{2,1,0:T(1,128)S(1)}, u32[]{:S(2)}, u32[]{:S(2)}) async-start(f32[32,1,2048]{2,1,0:T(1,128)} %broadcast_in_dim.88), calls=%async_computation | async-start | bytes 524288 | tf_op jit(solution)/shard_map/while/body/eval_jaxpr/all_to_all | solution.py:11
  404.2 13.2 %all-to-all-start = ((f32[32,1,2048]{2,1,0:T(1,128)}), f32[32,1,2048]{2,1,0:T(1,128)S(1)}, u32[]{:S(2)}, u32[]{:S(2)}) async-start(f32[32,1,2048]{2,1,0:T(1,128)} %broadcast_in_dim.88), calls=%async_computation | async-start | bytes 524288 | tf_op jit(solution)/shard_map/while/body/eval_jaxpr/all_to_all | solution.py:11
  433.4 13.2 %all-to-all-start = ((f32[32,1,2048]{2,1,0:T(1,128)}), f32[32,1,2048]{2,1,0:T(1,128)S(1)}, u32[]{:S(2)}, u32[]{:S(2)}) async-start(f32[32,1,2048]{2,1,0:T(1,128)} %broadcast_in_dim.88), calls=%async_computation | async-start | bytes 524288 | tf_op jit(solution)/shard_map/while/body/eval_jaxpr/all_to_all | solution.py:11
  462.6 13.2 %all-to-all-start = ((f32[32,1,2048]{2,1,0:T(1,128)}), f32[32,1,2048]{2,1,0:T(1,128)S(1)}, u32[]{:S(2)}, u32[]{:S(2)}) async-start(f32[32,1,2048]{2,1,0:T(1,128)} %broadcast_in_dim.88), calls=%async_computation | async-start | bytes 524288 | tf_op jit(solution)/shard_map/while/body/eval_jaxpr/all_to_all | solution.py:11
  491.7 13.2 %all-to-all-start = ((f32[32,1,2048]{2,1,0:T(1,128)}), f32[32,1,2048]{2,1,0:T(1,128)S(1)}, u32[]{:S(2)}, u32[]{:S(2)}) async-start(f32[32,1,2048]{2,1,0:T(1,128)} %broadcast_in_dim.88), calls=%async_computation | async-start | bytes 524288 | tf_op jit(solution)/shard_map/while/body/eval_jaxpr/all_to_all | solution.py:11
  520.9 13.2 %all-to-all-start = ((f32[32,1,2048]{2,1,0:T(1,128)}), f32[32,1,2048]{2,1,0:T(1,128)S(1)}, u32[]{:S(2)}, u32[]{:S(2)}) async-start(f32[32,1,2048]{2,1,0:T(1,128)} %broadcast_in_dim.88), calls=%async_computation | async-start | bytes 524288 | tf_op jit(solution)/shard_map/while/body/eval_jaxpr/all_to_all | solution.py:11
  550.0 13.2 %all-to-all-start = ((f32[32,1,2048]{2,1,0:T(1,128)}), f32[32,1,2048]{2,1,0:T(1,128)S(1)}, u32[]{:S(2)}, u32[]{:S(2)}) async-start(f32[32,1,2048]{2,1,0:T(1,128)} %broadcast_in_dim.88), calls=%async_computation | async-start | bytes 524288 | tf_op jit(solution)/shard_map/while/body/eval_jaxpr/all_to_all | solution.py:11
  (41 other events, 619.8 us)
Sparse Core Ops, SparseCore 0:
  577.2 137.3 all-reduce.4
where the time goes:
time: 729 us; the launch traced here: 724 us
  waiting for transfers between devices  275 us (38%)
  blocking collectives  120 us (16%)
  starting transfers between devices  115 us (16%)
  other arithmetic  108 us (15%)
  local copies, waits for them, and re-layouts  55.2 us (8%)
  matrix products  33.4 us (5%)
  between operations  14.1 us (2%)
    all_to_all x19, waiting for transfers between devices, from_everyone(): return lax.all_to_all(copies, axis, split_axis=0, concat_axis=0, tiled=True)  132 us
    ppermute x19, waiting for transfers between devices, shifted(): return lax.ppermute(x, axis, pairs)  127 us
    psum x1, blocking collectives, body(): lax.psum(kernel_acc.astype(jnp.bfloat16), 'dp').astype(jnp.float32)  120 us
    all_to_all x19, starting transfers between devices, from_everyone(): return lax.all_to_all(copies, axis, split_axis=0, concat_axis=0, tiled=True)  87.7 us
    dynamic_update_slice x19, other arithmetic, step(): grads_out = lax.dynamic_update_index_in_dim(grads_out, kept_grad, slot, 0)  37.7 us
    ppermute x19, starting transfers between devices, shifted(): return lax.ppermute(x, axis, pairs)  26.8 us
    dot_general x19, matrix products, step(): lax.dot_general(depth_slot, pre_grad, (((0,), (0,)), ((), ())), preferred...  25.6 us
    reduce_sum x19, other arithmetic, step(): jnp.sum(pre_slot, axis=0)  20 us
  transfers between devices with their start and end apart: 39, of which 39 were waited for; matrix products, arithmetic and copies ran while one was open for 9% of the time, Pallas kernels for 0%

commit v1 on v0

v1 whole, which is shorter than its diff:
```python
import functools

import jax
import jax.numpy as jnp
from jax import lax
from jax.experimental import pallas as pl
from jax.experimental.pallas import tpu as pltpu
from jax.sharding import PartitionSpec as P

MESH = pl.DeviceIdType.MESH
epsilon = 1e-05
LANES = 128


def columns_of(x, width):
    rows = x.shape[0]
    at = lax.broadcasted_iota(jnp.int32, x.shape, 0) % width
    before = jnp.where(at == 0, 0.0, pltpu.roll(x, 1, 0))
    after = jnp.where(at == width - 1, 0.0, pltpu.roll(x, rows - 1, 0))
    return before, x, after


def down(x, width):
    return jnp.concatenate([jnp.zeros((width, x.shape[1]), x.dtype), x[:-width]], axis=0)


def up(x, width):
    return jnp.concatenate([x[width:], jnp.zeros((width, x.shape[1]), x.dtype)], axis=0)


def kernel(
    sections, replicas, micros, height, width, channels,
    acts, out_grad, kern, weight, gain,
    out, point, kgrad, ggrad, bgrad,
    x_v, w_v, kf, depth, normed, nsend, nrecv, ubuf, usend, pgs, dgs,
    sbuf, smsg, omsg, tbuf, tmsg, stat, gacc,
    pacc, rs_src, rs_buf, ag_src, ag_buf, kacc, krs_buf, kag_src, kag_buf,
    in_sem, og_sem, out_sem,
    t_send, t_recv, n_send, n_recv, u_send, u_recv, s_send, s_recv, o_send,
    rs_send, rs_recv, ag_send, ag_recv, ks_send, ks_recv, kg_send, kg_recv,
):
    f32, bf16 = jnp.float32, jnp.bfloat16
    sec = lax.axis_index("section")
    me = lax.axis_index("dp")
    rows = height * width
    chunks = channels // LANES
    count = replicas * rows
    last = sections - 1
    below = (sec + sections - 1) % sections
    above = (sec + 1) % sections

    def lanes(c):
        return slice(c * LANES, (c + 1) * LANES)

    for m in range(micros):
        pltpu.make_async_copy(acts.at[0, m, 0], x_v.at[m], in_sem.at[m]).start()
        if m == 0:
            pltpu.make_async_copy(weight.at[0], w_v, in_sem.at[micros]).start()

    @pl.when(sec == last)
    def _():
        for m in range(micros):
            pltpu.make_async_copy(out_grad.at[m, 0], ubuf.at[m], og_sem.at[m]).start()

    barrier = pltpu.get_barrier_semaphore()

    def greet(k, _):
        peer = (me + k) % replicas
        pl.semaphore_signal(barrier, inc=1, device_id={"section": below, "dp": peer}, device_id_type=MESH)
        pl.semaphore_signal(barrier, inc=1, device_id={"section": above, "dp": peer}, device_id_type=MESH)

        @pl.when(k > 0)
        def _():
            pl.semaphore_signal(barrier, inc=1, device_id={"section": sec, "dp": peer}, device_id_type=MESH)

        return 0

    lax.fori_loop(0, replicas, greet, 0)

    for i in range(3):
        for j in range(3):
            kf[3 * i + j] = jnp.reshape(kern[0, i, j].astype(f32), (1, channels))
    kacc[...] = jnp.zeros(kacc.shape, f32)
    gacc[...] = jnp.zeros(gacc.shape, f32)
    pacc[...] = jnp.zeros(pacc.shape, f32)

    def tap(i, j, c):
        return kf[3 * i + j, :, lanes(c)]

    def to_plane(section, src, dst, send, recv, first):
        def one(k, _):
            peer = (me + k) % replicas
            pltpu.make_async_remote_copy(
                src_ref=src(peer), dst_ref=dst, send_sem=send, recv_sem=recv,
                device_id={"section": section, "dp": peer}, device_id_type=MESH,
            ).start()
            return 0

        lax.fori_loop(first, replicas, one, 0)

    def wait_bytes(ref, sem):
        pltpu.make_async_copy(ref, ref, sem).wait()

    def row_sum(x):
        return jnp.sum(x, axis=0, keepdims=True)

    def forward(m, _):
        pltpu.make_async_copy(acts.at[0, m, 0], x_v.at[m], in_sem.at[m]).wait()
        for c in range(chunks):
            x = x_v[m, :, :, lanes(c)].astype(f32).reshape(rows, LANES)
            parts = columns_of(jnp.maximum(x, 0.0), width)
            line = [sum(tap(i, j, c) * parts[j] for j in range(3)) for i in range(3)]
            depth[m, :, lanes(c)] = (down(line[0], width) + line[1] + up(line[2], width)).astype(bf16)

        @pl.when(m == 0)
        def _():
            pltpu.make_async_copy(weight.at[0], w_v, in_sem.at[micros]).wait()

        normed[m] = jnp.dot(depth[m], w_v[...], preferred_element_type=f32)
        for c in range(chunks):
            pre = normed[m, :, lanes(c)]
            tmsg[m, c : c + 1, :] = row_sum(pre)
            tmsg[m, chunks + c : chunks + c + 1, :] = row_sum(pre * pre)

        @pl.when(m == 0)
        def _():
            pl.semaphore_wait(barrier, 3 * replicas - 1)

        tbuf[m, me] = tmsg[m]
        to_plane(sec, lambda _: tmsg.at[m], tbuf.at[m, me], t_send, t_recv.at[m], 1)

        @pl.when(sec == last)
        def _():
            pltpu.make_async_copy(out_grad.at[m, 0], ubuf.at[m], og_sem.at[m]).wait()
            for c in range(chunks):
                u = ubuf[m, :, :, lanes(c)].astype(f32).reshape(rows, LANES)
                omsg[m, c : c + 1, :] = row_sum(u)
                omsg[m, chunks + c : chunks + c + 1, :] = row_sum(u * normed[m, :, lanes(c)])
            sbuf[m, me] = omsg[m]
            to_plane(sec, lambda _: omsg.at[m], sbuf.at[m, me], o_send, s_recv.at[m], 1)

        return 0

    lax.fori_loop(0, micros, forward, 0)

    def normalise(m, _):
        wait_bytes(tbuf.at[m, pl.ds(0, replicas - 1)], t_recv.at[m])
        total = jnp.sum(tbuf[m], axis=0) / count
        center = total[:chunks]
        inv_std = lax.rsqrt(total[chunks:] - center * center + epsilon)
        stat[m, 0:chunks, :] = center
        stat[m, chunks:, :] = inv_std
        for c in range(chunks):
            value = (normed[m, :, lanes(c)] - center[c : c + 1]) * inv_std[c : c + 1]
            normed[m, :, lanes(c)] = value
            nsend[m, :, lanes(c)] = value.astype(bf16)

        @pl.when(sec < last)
        def _():
            pltpu.make_async_remote_copy(
                src_ref=nsend.at[m], dst_ref=nrecv.at[m], send_sem=n_send, recv_sem=n_recv.at[m],
                device_id={"section": above, "dp": me}, device_id_type=MESH,
            ).start()

        return 0

    lax.fori_loop(0, micros, normalise, 0)

    def backward(m, _):
        @pl.when(sec == last)
        def _():
            wait_bytes(sbuf.at[m, pl.ds(0, replicas - 1)], s_recv.at[m])

        @pl.when(sec < last)
        def _():
            wait_bytes(sbuf.at[m], s_recv.at[m])
            wait_bytes(ubuf.at[m], u_recv.at[m])

        total = jnp.sum(sbuf[m], axis=0)
        center, inv_std = stat[m, 0:chunks, :], stat[m, chunks:, :]
        sum_grad, cross = total[:chunks], total[chunks:]
        cross = jnp.where(sec == last, inv_std * (cross - center * sum_grad), cross)
        gacc[0:chunks, :] += sum_grad
        gacc[chunks:, :] += cross
        for c in range(chunks):
            scale = gain[0:1, lanes(c)] * inv_std[c : c + 1]
            shift = scale * sum_grad[c : c + 1] / count
            slope = scale * cross[c : c + 1] / count
            u = ubuf[m, :, :, lanes(c)].astype(f32).reshape(rows, LANES)
            pgs[:, lanes(c)] = (scale * u - shift - slope * normed[m, :, lanes(c)]).astype(bf16)
        dgs[...] = lax.dot_general(pgs[...], w_v[...], (((1,), (1,)), ((), ())), preferred_element_type=f32)

        @pl.when(sec > 0)
        def _():
            wait_bytes(nrecv.at[m], n_recv.at[m])

        for c in range(chunks):
            after, same, before = columns_of(dgs[:, lanes(c)], width)[::-1]
            parts = (after, same, before)
            line = [sum(tap(i, j, c) * parts[j] for j in range(3)) for i in range(3)]
            back = up(line[0], width) + line[1] + down(line[2], width)
            u = ubuf[m, :, :, lanes(c)].astype(f32).reshape(rows, LANES)
            x = x_v[m, :, :, lanes(c)].astype(f32).reshape(rows, LANES)
            result = (u + jnp.where(x > 0, back, 0.0)).astype(bf16)
            usend[m, :, :, lanes(c)] = result.reshape(height, width, LANES)

            @pl.when(sec > 0)
            def _():
                pltpu.make_async_remote_copy(
                    src_ref=usend.at[m, :, :, pl.ds(c * LANES, LANES)],
                    dst_ref=ubuf.at[m, :, :, pl.ds(c * LANES, LANES)],
                    send_sem=u_send, recv_sem=u_recv.at[m],
                    device_id={"section": below, "dp": me}, device_id_type=MESH,
                ).start()

            wide = result.astype(f32)
            smsg[m, c : c + 1, :] = row_sum(wide)
            smsg[m, chunks + c : chunks + c + 1, :] = row_sum(wide * nrecv[m, :, lanes(c)].astype(f32))

        @pl.when(sec > 0)
        def _():
            to_plane(below, lambda _: smsg.at[m], sbuf.at[m, me], s_send, s_recv.at[m], 0)

        pltpu.make_async_copy(usend.at[m], out.at[0, m, 0], out_sem.at[m]).start()

        pacc[...] += lax.dot_general(
            depth[m], pgs[...], (((0,), (0,)), ((), ())), preferred_element_type=f32
        )
        for c in range(chunks):
            x = x_v[m, :, :, lanes(c)].astype(f32).reshape(rows, LANES)
            active = jnp.maximum(x, 0.0)
            parts = columns_of(dgs[:, lanes(c)], width)[::-1]
            per = kacc.shape[1]
            for i in range(3):
                for j in range(3):
                    moved = (up(parts[j], width), parts[j], down(parts[j], width))[i]
                    r = (3 * i + j) * chunks + c
                    kacc[r // per, r % per : r % per + 1, :] += row_sum(active * moved)
        return 0

    @pl.when(sec == 0)
    def _():
        nrecv[...] = jnp.zeros(nrecv.shape, bf16)

    lax.fori_loop(0, micros, backward, 0)

    for c in range(chunks):
        bgrad[0:1, lanes(c)] = gacc[c : c + 1, :]
        ggrad[0:1, lanes(c)] = gacc[chunks + c : chunks + c + 1, :]

    rs_src[...] = pacc[...].reshape(rs_src.shape).astype(bf16)
    to_plane(sec, lambda peer: rs_src.at[peer], rs_buf.at[me], rs_send, rs_recv, 1)
    to_plane(sec, lambda peer: kacc.at[peer], krs_buf.at[me], ks_send, ks_recv, 1)
    rs_buf[me] = rs_src[me]
    krs_buf[me] = kacc[me]
    wait_bytes(rs_buf.at[pl.ds(0, replicas - 1)], rs_recv)
    ag_src[...] = jnp.sum(rs_buf[...].astype(f32), axis=0).astype(bf16)
    to_plane(sec, lambda _: ag_src, ag_buf.at[me], ag_send, ag_recv, 1)
    wait_bytes(krs_buf.at[pl.ds(0, replicas - 1)], ks_recv)
    kag_src[...] = jnp.sum(krs_buf[...], axis=0)
    to_plane(sec, lambda _: kag_src, kag_buf.at[me], kg_send, kg_recv, 1)
    ag_buf[me] = ag_src[...]
    kag_buf[me] = kag_src[...]
    wait_bytes(kag_buf.at[pl.ds(0, replicas - 1)], kg_recv)
    per = kacc.shape[1]
    for t in range(9):
        for c in range(chunks):
            r = t * chunks + c
            kgrad[0, t // 3, t % 3 : t % 3 + 1, lanes(c)] = kag_buf[r // per, r % per : r % per + 1, :]
    wait_bytes(ag_buf.at[pl.ds(0, replicas - 1)], ag_recv)
    point[0] = ag_buf[...].astype(f32).reshape(channels, channels)

    for m in range(micros):
        pltpu.make_async_copy(usend.at[m], out.at[0, m, 0], out_sem.at[m]).wait()
    wait_bytes(tbuf.at[:, pl.ds(0, replicas - 1)], t_send)

    @pl.when(sec < last)
    def _():
        wait_bytes(nsend, n_send)

    @pl.when(sec == last)
    def _():
        wait_bytes(sbuf.at[:, pl.ds(0, replicas - 1)], o_send)

    @pl.when(sec > 0)
    def _():
        wait_bytes(usend, u_send)
        wait_bytes(sbuf, s_send)

    wait_bytes(rs_buf.at[pl.ds(0, replicas - 1)], rs_send)
    wait_bytes(krs_buf.at[pl.ds(0, replicas - 1)], ks_send)
    wait_bytes(ag_buf.at[pl.ds(0, replicas - 1)], ag_send)
    wait_bytes(kag_buf.at[pl.ds(0, replicas - 1)], kg_send)


def solution(mesh):
    sections, replicas = mesh.shape["section"], mesh.shape["dp"]

    def body(acts, out_grad, depth_kernel, point_weight, bn_gain):
        micros, _, height, width, channels = acts.shape[1:]
        rows = height * width
        chunks = channels // LANES
        share = channels // replicas
        per = -(-9 * chunks // replicas)
        f32, bf16 = jnp.float32, jnp.bfloat16
        image = (micros, height, width, channels)
        flat = (micros, rows, channels)
        vmem, dma = pltpu.VMEM, pltpu.SemaphoreType.DMA
        any_space = pl.BlockSpec(memory_space=pl.ANY)
        in_vmem = pl.BlockSpec(memory_space=pltpu.VMEM)
        return pl.pallas_call(
            functools.partial(kernel, sections, replicas, micros, height, width, channels),
            out_shape=(
                jax.ShapeDtypeStruct(acts.shape, bf16),
                jax.ShapeDtypeStruct((1, channels, channels), f32),
                jax.ShapeDtypeStruct((1, 3, 3, channels), f32),
                jax.ShapeDtypeStruct((1, channels), f32),
                jax.ShapeDtypeStruct((1, channels), f32),
            ),
            in_specs=[any_space, any_space, in_vmem, any_space, in_vmem],
            out_specs=(any_space, in_vmem, in_vmem, in_vmem, in_vmem),
            scratch_shapes=[
                vmem(image, bf16), vmem((channels, channels), bf16), vmem((9, 1, channels), f32),
                vmem(flat, bf16), vmem(flat, f32), vmem(flat, bf16), vmem(flat, bf16),
                vmem(image, bf16), vmem(image, bf16), vmem((rows, channels), bf16), vmem((rows, channels), f32),
                vmem((micros, replicas, 2 * chunks, LANES), f32), vmem((micros, 2 * chunks, LANES), f32),
                vmem((micros, 2 * chunks, LANES), f32),
                vmem((micros, replicas, 2 * chunks, LANES), f32), vmem((micros, 2 * chunks, LANES), f32),
                vmem((micros, 2 * chunks, LANES), f32), vmem((2 * chunks, LANES), f32),
                vmem((channels, channels), f32),
                vmem((replicas, share, channels), bf16), vmem((replicas, share, channels), bf16),
                vmem((share, channels), bf16), vmem((replicas, share, channels), bf16),
                vmem((replicas, per, LANES), f32), vmem((replicas, per, LANES), f32),
                vmem((per, LANES), f32), vmem((replicas, per, LANES), f32),
                dma((micros + 1,)), dma((micros,)), dma((micros,)),
                dma, dma((micros,)), dma, dma((micros,)), dma, dma((micros,)), dma, dma((micros,)), dma,
                dma, dma, dma, dma, dma, dma, dma, dma,
            ],
            compiler_params=pltpu.CompilerParams(collective_id=0, has_side_effects=True),
        )(acts, out_grad, depth_kernel, point_weight, bn_gain)

    return jax.shard_map(
        body,
        mesh=mesh,
        in_specs=(
            P("section", None, "dp", None, None, None),
            P(None, "dp", None, None, None),
            P("section", None, None, None),
            P("section", None, None),
            P("section", None),
        ),
        out_specs=(
            P("section", None, "dp", None, None, None),
            P("section", None, None),
            P("section", None, None, None),
            P("section", None),
            P("section", None),
        ),
        check_vma=False,
    )
```

time: 729 us -> 251 us (0.34)
  waiting for transfers between devices: 275 us -> 0 us
  Pallas kernels: 0 us -> 244 us
  blocking collectives: 120 us -> 0 us
  starting transfers between devices: 115 us -> 0 us
  other arithmetic: 108 us -> 0 us
  local copies, waits for them, and re-layouts: 55.2 us -> 5.74 us
  matrix products: 33.4 us -> 0 us
  between operations: 14.1 us -> 0.65 us
    pallas_call x0 -> x1, Pallas kernels: none -> 244 us  [body(): pl.pallas_call(functools.partial(kernel, sections, replicas, micros, heig...]
    all_to_all x19 -> x0, waiting for transfers between devices: 132 us -> none  [from_everyone(): return lax.all_to_all(copies, axis, split_axis=0, concat_axis=0, tiled=True)]
    ppermute x19 -> x0, waiting for transfers between devices: 127 us -> none  [shifted(): return lax.ppermute(x, axis, pairs)]
    psum x1 -> x0, blocking collectives: 120 us -> none  [body(): lax.psum(kernel_acc.astype(jnp.bfloat16), 'dp').astype(jnp.float32)]
    all_to_all x19 -> x0, starting transfers between devices: 87.7 us -> none  [from_everyone(): return lax.all_to_all(copies, axis, split_axis=0, concat_axis=0, tiled=True)]
    reduce_sum x95 -> x0, other arithmetic: 50 us -> none  [the longest x19 20 us: step(): jnp.sum(pre_slot, axis=0)]
    dynamic_update_slice x19 -> x0, other arithmetic: 37.7 us -> none  [step(): grads_out = lax.dynamic_update_index_in_dim(grads_out, kept_grad, slot, 0)]
    dot_general x39 -> x0, matrix products: 33.4 us -> none  [the longest x19 25.6 us: step(): lax.dot_general(depth_slot, pre_grad, (((0,), (0,)), ((), ())), preferred...]
  transfers between devices with their start and end apart: 39 -> 0, of which waited for: 39 -> 0; matrix products, arithmetic and copies ran while one was open for 9% -> 0% of each run, Pallas kernels for 0% -> 0%
where the time goes in v1:
time: 251 us; the launch traced here: 250 us
  Pallas kernels  244 us (97%)
  local copies, waits for them, and re-layouts  5.74 us (2%)
    pallas_call x1, Pallas kernels, body(): pl.pallas_call(functools.partial(kernel, sections, replicas, micros, heig...  244 us

profile of v1, /device:TPU:1, one launch (start us, length us, event | category | flops | bytes accessed | tf_op | source)
XLA Modules:
  0.0 250.3 jit_solution(9185934372597221911)
XLA Ops:
  0.6 243.9 %shard_map.92 = (bf16[1,4,1,12,16,512]{5,4,3,2,1,0:T(8,128)(2,1)}, f32[1,512,512]{2,1,0:T(8,128)}, f32[1,3,3,512]{3,2,1,0:T(4,128)}, f32[1,512]{1,0:T(1,128)}, f32[1,512]{1,0:T(1,128)}) custom-call(bf16[1,4,1,12,16,512]{5,4,3,2,1,0:T(8,128)(2,1)} %acts.1, bf16[4,1,12,16,512]{4,3,2,1,0:T(8,128)(2,1)} %out_grad.1, bf16[1,3,3,512]{3,2,1,0:T(4,128)(2,1)} %kern.1, ...), custom_call_target="tpu_custom_call" | custom-call | tf_op jit(solution)/shard_map/pallas_call | solution.py:311
  244.6 0.0 copy-start
  244.6 1.4 copy.10
  246.0 2.1 copy.15
  248.1 0.0 copy-done
  248.1 0.0 copy-start.2
  248.1 1.0 copy.16
  249.1 0.0 copy-done.2
  249.1 0.0 copy-start.1
  249.1 0.6 copy.17
  249.7 0.1 copy-done.1
  249.8 0.6 copy.18
Async XLA Ops:
  244.6 3.5 %copy-start = (f32[1,512,512]{2,1,0:T(8,128)S(1)}, f32[1,512,512]{2,1,0:T(8,128)}, u32[]{:S(2)}) copy-start(f32[1,512,512]{2,1,0:T(8,128)} %get-tuple-element.16) | copy-start | bytes 3145732
  248.1 1.0 copy-start.2
  249.1 0.7 copy-start.1

commit v2 on v1

--- a/solution.py
+++ b/solution.py
@@ -33,10 +33,11 @@
     acts, out_grad, kern, weight, gain,
     out, point, kgrad, ggrad, bgrad,
     x_v, w_v, kf, depth, normed, nsend, nrecv, ubuf, usend, pgs, dgs,
-    sbuf, smsg, omsg, tbuf, tmsg, stat, gacc,
+    ones, lows, base, cmsg, crecv,
+    sbuf, fmsg, pbuf, smsg, obuf, omsg, tbuf, tmsg, stat, gacc,
     pacc, rs_src, rs_buf, ag_src, ag_buf, kacc, krs_buf, kag_src, kag_buf,
     in_sem, og_sem, out_sem,
-    t_send, t_recv, n_send, n_recv, u_send, u_recv, s_send, s_recv, o_send,
+    t_send, t_recv, n_send, n_recv, c_send, c_recv, u_send, u_recv, p_send, p_recv, f_send, s_recv, o_send, o_recv,
     rs_send, rs_recv, ag_send, ag_recv, ks_send, ks_recv, kg_send, kg_recv,
 ):
     f32, bf16 = jnp.float32, jnp.bfloat16
@@ -87,6 +88,11 @@
     def tap(i, j, c):
         return kf[3 * i + j, :, lanes(c)]
 
+    def convolve(x, c):
+        parts = columns_of(x, width)
+        line = [sum(tap(i, j, c) * parts[j] for j in range(3)) for i in range(3)]
+        return down(line[0], width) + line[1] + up(line[2], width)
+
     def to_plane(section, src, dst, send, recv, first):
         def one(k, _):
             peer = (me + k) % replicas
@@ -108,9 +114,7 @@
         pltpu.make_async_copy(acts.at[0, m, 0], x_v.at[m], in_sem.at[m]).wait()
         for c in range(chunks):
             x = x_v[m, :, :, lanes(c)].astype(f32).reshape(rows, LANES)
-            parts = columns_of(jnp.maximum(x, 0.0), width)
-            line = [sum(tap(i, j, c) * parts[j] for j in range(3)) for i in range(3)]
-            depth[m, :, lanes(c)] = (down(line[0], width) + line[1] + up(line[2], width)).astype(bf16)
+            depth[m, :, lanes(c)] = convolve(jnp.maximum(x, 0.0), c).astype(bf16)
 
         @pl.when(m == 0)
         def _():
@@ -121,13 +125,23 @@
             pre = normed[m, :, lanes(c)]
             tmsg[m, c : c + 1, :] = row_sum(pre)
             tmsg[m, chunks + c : chunks + c + 1, :] = row_sum(pre * pre)
+            cmsg[m, c : c + 1, :] = tmsg[m, c : c + 1, :] / rows
+            nsend[m, :, lanes(c)] = (pre - cmsg[m, c : c + 1, :]).astype(bf16)
 
         @pl.when(m == 0)
         def _():
             pl.semaphore_wait(barrier, 3 * replicas - 1)
 
+        to_plane(sec, lambda _: tmsg.at[m], tbuf.at[m, me], t_send, t_recv.at[m], 1)
         tbuf[m, me] = tmsg[m]
-        to_plane(sec, lambda _: tmsg.at[m], tbuf.at[m, me], t_send, t_recv.at[m], 1)
+
+        @pl.when(sec < last)
+        def _():
+            for src, dst, send, recv in ((cmsg, crecv, c_send, c_recv), (nsend, nrecv, n_send, n_recv)):
+                pltpu.make_async_remote_copy(
+                    src_ref=src.at[m], dst_ref=dst.at[m], send_sem=send, recv_sem=recv.at[m],
+                    device_id={"section": above, "dp": me}, device_id_type=MESH,
+                ).start()
 
         @pl.when(sec == last)
         def _():
@@ -136,50 +150,58 @@
                 u = ubuf[m, :, :, lanes(c)].astype(f32).reshape(rows, LANES)
                 omsg[m, c : c + 1, :] = row_sum(u)
                 omsg[m, chunks + c : chunks + c + 1, :] = row_sum(u * normed[m, :, lanes(c)])
-            sbuf[m, me] = omsg[m]
-            to_plane(sec, lambda _: omsg.at[m], sbuf.at[m, me], o_send, s_recv.at[m], 1)
+            to_plane(sec, lambda _: omsg.at[m], obuf.at[m, me], o_send, o_recv.at[m], 1)
+            obuf[m, me] = omsg[m]
 
         return 0
 
     lax.fori_loop(0, micros, forward, 0)
 
-    def normalise(m, _):
+    def prepare(m):
         wait_bytes(tbuf.at[m, pl.ds(0, replicas - 1)], t_recv.at[m])
         total = jnp.sum(tbuf[m], axis=0) / count
         center = total[:chunks]
         inv_std = lax.rsqrt(total[chunks:] - center * center + epsilon)
-        stat[m, 0:chunks, :] = center
-        stat[m, chunks:, :] = inv_std
-        for c in range(chunks):
-            value = (normed[m, :, lanes(c)] - center[c : c + 1]) * inv_std[c : c + 1]
-            normed[m, :, lanes(c)] = value
-            nsend[m, :, lanes(c)] = value.astype(bf16)
-
+        stat[0:chunks, :] = center
+        stat[chunks:, :] = inv_std
+        for c in range(chunks):
+            normed[m, :, lanes(c)] = (normed[m, :, lanes(c)] - center[c : c + 1]) * inv_std[c : c + 1]
+
+        @pl.when(sec > 0)
+        def _():
+            wait_bytes(nrecv.at[m], n_recv.at[m])
+            wait_bytes(crecv.at[m], c_recv.at[m])
+            for c in range(chunks):
+                x = x_v[m, :, :, lanes(c)].astype(f32).reshape(rows, LANES)
+                low = nrecv[m, :, lanes(c)].astype(f32)
+                ones[:, lanes(c)] = convolve(jnp.where(x > 0, 1.0, 0.0), c)
+                lows[:, lanes(c)] = convolve(jnp.where(x > 0, low, 0.0), c)
+
+    def critical(m):
         @pl.when(sec < last)
         def _():
-            pltpu.make_async_remote_copy(
-                src_ref=nsend.at[m], dst_ref=nrecv.at[m], send_sem=n_send, recv_sem=n_recv.at[m],
-                device_id={"section": above, "dp": me}, device_id_type=MESH,
-            ).start()
-
-        return 0
-
-    lax.fori_loop(0, micros, normalise, 0)
-
-    def backward(m, _):
+            wait_bytes(ubuf.at[m], u_recv.at[m])
+
+        @pl.when(sec > 0)
+        def _():
+            for c in range(chunks):
+                u = ubuf[m, :, :, lanes(c)].astype(f32).reshape(rows, LANES)
+                base[c : c + 1, :] = row_sum(u)
+                base[chunks + c : chunks + c + 1, :] = row_sum(u * nrecv[m, :, lanes(c)].astype(f32))
+
         @pl.when(sec == last)
         def _():
-            wait_bytes(sbuf.at[m, pl.ds(0, replicas - 1)], s_recv.at[m])
+            wait_bytes(obuf.at[m, pl.ds(0, replicas - 1)], o_recv.at[m])
+            sbuf[m] = jnp.sum(obuf[m], axis=0)
 
         @pl.when(sec < last)
         def _():
             wait_bytes(sbuf.at[m], s_recv.at[m])
-            wait_bytes(ubuf.at[m], u_recv.at[m])
-
-        total = jnp.sum(sbuf[m], axis=0)
-        center, inv_std = stat[m, 0:chunks, :], stat[m, chunks:, :]
-        sum_grad, cross = total[:chunks], total[chunks:]
-        cross = jnp.where(sec == last, inv_std * (cross - center * sum_grad), cross)
+
+        total = sbuf[m]
+        center, inv_std = stat[0:chunks, :], stat[chunks:, :]
+        sum_grad = total[:chunks]
+        cross = inv_std * (total[chunks:] - center * sum_grad)
         gacc[0:chunks, :] += sum_grad
         gacc[chunks:, :] += cross
         for c in range(chunks):
@@ -192,11 +214,17 @@
 
         @pl.when(sec > 0)
         def _():
-            wait_bytes(nrecv.at[m], n_recv.at[m])
-
-        for c in range(chunks):
-            after, same, before = columns_of(dgs[:, lanes(c)], width)[::-1]
-            parts = (after, same, before)
+            for c in range(chunks):
+                grad = dgs[:, lanes(c)]
+                plain = base[c : c + 1, :] + row_sum(grad * ones[:, lanes(c)])
+                mixed = base[chunks + c : chunks + c + 1, :] + row_sum(grad * lows[:, lanes(c)])
+                smsg[m, c : c + 1, :] = plain
+                smsg[m, chunks + c : chunks + c + 1, :] = mixed + crecv[m, c : c + 1, :] * plain
+            to_plane(sec, lambda _: smsg.at[m], pbuf.at[m, me], p_send, p_recv.at[m], 1)
+            pbuf[m, me] = smsg[m]
+
+        for c in range(chunks):
+            parts = columns_of(dgs[:, lanes(c)], width)[::-1]
             line = [sum(tap(i, j, c) * parts[j] for j in range(3)) for i in range(3)]
             back = up(line[0], width) + line[1] + down(line[2], width)
             u = ubuf[m, :, :, lanes(c)].astype(f32).reshape(rows, LANES)
@@ -213,34 +241,39 @@
                     device_id={"section": below, "dp": me}, device_id_type=MESH,
                 ).start()
 
-            wide = result.astype(f32)
-            smsg[m, c : c + 1, :] = row_sum(wide)
-            smsg[m, chunks + c : chunks + c + 1, :] = row_sum(wide * nrecv[m, :, lanes(c)].astype(f32))
-
+        pltpu.make_async_copy(usend.at[m], out.at[0, m, 0], out_sem.at[m]).start()
+
+    def hand_down(m):
         @pl.when(sec > 0)
         def _():
-            to_plane(below, lambda _: smsg.at[m], sbuf.at[m, me], s_send, s_recv.at[m], 0)
-
-        pltpu.make_async_copy(usend.at[m], out.at[0, m, 0], out_sem.at[m]).start()
-
+            wait_bytes(pbuf.at[m, pl.ds(0, replicas - 1)], p_recv.at[m])
+            fmsg[m] = jnp.sum(pbuf[m], axis=0)
+            pltpu.make_async_remote_copy(
+                src_ref=fmsg.at[m], dst_ref=sbuf.at[m], send_sem=f_send, recv_sem=s_recv.at[m],
+                device_id={"section": below, "dp": me}, device_id_type=MESH,
+            ).start()
+
+    def weights(m):
         pacc[...] += lax.dot_general(
             depth[m], pgs[...], (((0,), (0,)), ((), ())), preferred_element_type=f32
         )
+        per = kacc.shape[1]
         for c in range(chunks):
             x = x_v[m, :, :, lanes(c)].astype(f32).reshape(rows, LANES)
             active = jnp.maximum(x, 0.0)
             parts = columns_of(dgs[:, lanes(c)], width)[::-1]
-            per = kacc.shape[1]
             for i in range(3):
                 for j in range(3):
                     moved = (up(parts[j], width), parts[j], down(parts[j], width))[i]
                     r = (3 * i + j) * chunks + c
                     kacc[r // per, r % per : r % per + 1, :] += row_sum(active * moved)
+
+    def backward(m, _):
+        prepare(m)
+        critical(m)
+        weights(m)
+        hand_down(m)
         return 0
-
-    @pl.when(sec == 0)
-    def _():
-        nrecv[...] = jnp.zeros(nrecv.shape, bf16)
 
     lax.fori_loop(0, micros, backward, 0)
 
@@ -268,7 +301,7 @@
             r = t * chunks + c
             kgrad[0, t // 3, t % 3 : t % 3 + 1, lanes(c)] = kag_buf[r // per, r % per : r % per + 1, :]
     wait_bytes(ag_buf.at[pl.ds(0, replicas - 1)], ag_recv)
-    point[0] = ag_buf[...].astype(f32).reshape(channels, channels)
+    point[0] = ag_buf[...].reshape(channels, channels)
 
     for m in range(micros):
         pltpu.make_async_copy(usend.at[m], out.at[0, m, 0], out_sem.at[m]).wait()
@@ -277,15 +310,17 @@
     @pl.when(sec < last)
     def _():
         wait_bytes(nsend, n_send)
+        wait_bytes(cmsg, c_send)
 
     @pl.when(sec == last)
     def _():
-        wait_bytes(sbuf.at[:, pl.ds(0, replicas - 1)], o_send)
+        wait_bytes(obuf.at[:, pl.ds(0, replicas - 1)], o_send)
 
     @pl.when(sec > 0)
     def _():
         wait_bytes(usend, u_send)
-        wait_bytes(sbuf, s_send)
+        wait_bytes(pbuf.at[:, pl.ds(0, replicas - 1)], p_send)
+        wait_bytes(fmsg, f_send)
 
     wait_bytes(rs_buf.at[pl.ds(0, replicas - 1)], rs_send)
     wait_bytes(krs_buf.at[pl.ds(0, replicas - 1)], ks_send)
@@ -305,14 +340,15 @@
         f32, bf16 = jnp.float32, jnp.bfloat16
         image = (micros, height, width, channels)
         flat = (micros, rows, channels)
+        sums = (2 * chunks, LANES)
         vmem, dma = pltpu.VMEM, pltpu.SemaphoreType.DMA
         any_space = pl.BlockSpec(memory_space=pl.ANY)
         in_vmem = pl.BlockSpec(memory_space=pltpu.VMEM)
-        return pl.pallas_call(
+        grads, point, kgrad, ggrad, bgrad = pl.pallas_call(
             functools.partial(kernel, sections, replicas, micros, height, width, channels),
             out_shape=(
                 jax.ShapeDtypeStruct(acts.shape, bf16),
-                jax.ShapeDtypeStruct((1, channels, channels), f32),
+                jax.ShapeDtypeStruct((1, channels, channels), bf16),
                 jax.ShapeDtypeStruct((1, 3, 3, channels), f32),
                 jax.ShapeDtypeStruct((1, channels), f32),
                 jax.ShapeDtypeStruct((1, channels), f32),
@@ -323,21 +359,25 @@
                 vmem(image, bf16), vmem((channels, channels), bf16), vmem((9, 1, channels), f32),
                 vmem(flat, bf16), vmem(flat, f32), vmem(flat, bf16), vmem(flat, bf16),
                 vmem(image, bf16), vmem(image, bf16), vmem((rows, channels), bf16), vmem((rows, channels), f32),
-                vmem((micros, replicas, 2 * chunks, LANES), f32), vmem((micros, 2 * chunks, LANES), f32),
-                vmem((micros, 2 * chunks, LANES), f32),
-                vmem((micros, replicas, 2 * chunks, LANES), f32), vmem((micros, 2 * chunks, LANES), f32),
-                vmem((micros, 2 * chunks, LANES), f32), vmem((2 * chunks, LANES), f32),
+                vmem((rows, channels), f32), vmem((rows, channels), f32), vmem(sums, f32),
+                vmem((micros, chunks, LANES), f32), vmem((micros, chunks, LANES), f32),
+                vmem((micros, *sums), f32), vmem((micros, *sums), f32),
+                vmem((micros, replicas, *sums), f32), vmem((micros, *sums), f32),
+                vmem((micros, replicas, *sums), f32), vmem((micros, *sums), f32),
+                vmem((micros, replicas, *sums), f32), vmem((micros, *sums), f32),
+                vmem(sums, f32), vmem(sums, f32),
                 vmem((channels, channels), f32),
                 vmem((replicas, share, channels), bf16), vmem((replicas, share, channels), bf16),
                 vmem((share, channels), bf16), vmem((replicas, share, channels), bf16),
                 vmem((replicas, per, LANES), f32), vmem((replicas, per, LANES), f32),
                 vmem((per, LANES), f32), vmem((replicas, per, LANES), f32),
                 dma((micros + 1,)), dma((micros,)), dma((micros,)),
-                dma, dma((micros,)), dma, dma((micros,)), dma, dma((micros,)), dma, dma((micros,)), dma,
+                *[dma, dma((micros,))] * 7,
                 dma, dma, dma, dma, dma, dma, dma, dma,
             ],
             compiler_params=pltpu.CompilerParams(collective_id=0, has_side_effects=True),
         )(acts, out_grad, depth_kernel, point_weight, bn_gain)
+        return grads, point.astype(f32), kgrad, ggrad, bgrad
 
     return jax.shard_map(
         body,

time: 251 us -> 196 us (0.78)
  Pallas kernels: 244 us -> 189 us
    pallas_call x1, Pallas kernels: 244 us -> 189 us  [body(): pl.pallas_call(functools.partial(kernel, sections, replicas, micros, heig...]
where the time goes in v2:
time: 196 us
  Pallas kernels  189 us (96%)
  local copies, waits for them, and re-layouts  3.5 us (2%)
  other arithmetic  2.22 us (1%)
    pallas_call x1, Pallas kernels, body(): pl.pallas_call(functools.partial(kernel, sections, replicas, micros, heig...  189 us

profile of v2, /device:TPU:1, one launch (start us, length us, event | category | flops | bytes accessed | tf_op | source)
XLA Modules:
  0.0 195.6 jit_solution(9581196789212168554)
XLA Ops:
  0.6 189.2 %shard_map.92 = (bf16[1,4,1,12,16,512]{5,4,3,2,1,0:T(8,128)(2,1)}, bf16[1,512,512]{2,1,0:T(8,128)(2,1)}, f32[1,3,3,512]{3,2,1,0:T(4,128)}, f32[1,512]{1,0:T(1,128)}, f32[1,512]{1,0:T(1,128)}) custom-call(bf16[1,4,1,12,16,512]{5,4,3,2,1,0:T(8,128)(2,1)} %acts.1, bf16[4,1,12,16,512]{4,3,2,1,0:T(8,128)(2,1)} %out_grad.1, bf16[1,3,3,512]{3,2,1,0:T(4,128)(2,1)} %kern.1, ...), custom_call_target="tpu_custom_call" | custom-call | tf_op jit(solution)/shard_map/pallas_call | solution.py:347
  189.9 1.4 copy.10
  191.2 0.0 copy-start
  191.2 2.2 %convert_element_type.3 = f32[1,512,512]{2,1,0:T(8,128)} convert(bf16[1,512,512]{2,1,0:T(8,128)(2,1)} %get-tuple-element.11) | non-fusion elementwise | flops 262144 | bytes 1572864 | tf_op jit(solution)/shard_map/convert_element_type | solution.py:380
  193.5 0.0 copy-done
  193.5 0.0 copy-start.2
  193.5 0.9 copy.14
  194.3 0.0 copy-done.2
  194.3 0.0 copy-start.1
  194.3 0.6 copy.15
  194.9 0.1 copy-done.1
  195.0 0.6 copy.16
Async XLA Ops:
  191.2 2.2 %copy-start = (bf16[1,4,1,12,16,512]{5,4,3,2,1,0:T(8,128)(2,1)S(1)}, bf16[1,4,1,12,16,512]{5,4,3,2,1,0:T(8,128)(2,1)}, u32[]{:S(2)}) copy-start(bf16[1,4,1,12,16,512]{5,4,3,2,1,0:T(8,128)(2,1)} %get-tuple-element.25) | copy-start | bytes 2359300
  193.5 0.9 copy-start.2
  194.3 0.7 copy-start.1

commit v3 on v2

--- a/solution.py
+++ b/solution.py
@@ -10,6 +10,7 @@
 MESH = pl.DeviceIdType.MESH
 epsilon = 1e-05
 LANES = 128
+REACH = 2
 
 
 def columns_of(x, width):
@@ -28,17 +29,29 @@
     return jnp.concatenate([x[width:], jnp.zeros((width, x.shape[1]), x.dtype)], axis=0)
 
 
+def ring(a, n):
+    return min(a, n - a)
+
+
+def offsets(ys, xs, reach):
+    every = [(y, x, c) for y in range(ys) for x in range(xs) for c in range(2) if (y, x, c) != (0, 0, 0)]
+    every.sort(key=lambda o: -(ring(o[0], ys) + ring(o[1], xs)))
+    far = [o for o in every if ring(o[0], ys) + ring(o[1], xs) > reach]
+    return far, [o for o in every if o not in far]
+
+
 def kernel(
+    ys, xs, far, near,
     sections, replicas, micros, height, width, channels,
     acts, out_grad, kern, weight, gain,
     out, point, kgrad, ggrad, bgrad,
     x_v, w_v, kf, depth, normed, nsend, nrecv, ubuf, usend, pgs, dgs,
     ones, lows, base, cmsg, crecv,
-    sbuf, fmsg, pbuf, smsg, obuf, omsg, tbuf, tmsg, stat, gacc,
-    pacc, rs_src, rs_buf, ag_src, ag_buf, kacc, krs_buf, kag_src, kag_buf,
+    dmsg, dbuf, sbuf, fmsg, pbuf, smsg, obuf, omsg, tbuf, tmsg, stat, gacc,
+    pacc, pair_src, pair_buf, rs_src, rs_buf, ag_src, ag_buf, kacc, krs_buf, kag_src, kag_buf,
     in_sem, og_sem, out_sem,
     t_send, t_recv, n_send, n_recv, c_send, c_recv, u_send, u_recv, p_send, p_recv, f_send, s_recv, o_send, o_recv,
-    rs_send, rs_recv, ag_send, ag_recv, ks_send, ks_recv, kg_send, kg_recv,
+    d_send, d_recv, w_send, w_recv, rs_send, rs_recv, ag_send, ag_recv, m_send, m_recv, ks_send, ks_recv, kg_send, kg_recv,
 ):
     f32, bf16 = jnp.float32, jnp.bfloat16
     sec = lax.axis_index("section")
@@ -93,6 +106,18 @@
         line = [sum(tap(i, j, c) * parts[j] for j in range(3)) for i in range(3)]
         return down(line[0], width) + line[1] + up(line[2], width)
 
+    core, at_x, at_y = me % 2, (me // 2) % xs, me // (2 * xs)
+
+    def device_at(offset):
+        dy, dx, dc = offset
+        return (((at_y + dy) % ys) * xs + (at_x + dx) % xs) * 2 + (core + dc) % 2
+
+    def to_peer(src, dst, send, recv, section, peer):
+        pltpu.make_async_remote_copy(
+            src_ref=src, dst_ref=dst, send_sem=send, recv_sem=recv,
+            device_id={"section": section, "dp": peer}, device_id_type=MESH,
+        ).start()
+
     def to_plane(section, src, dst, send, recv, first):
         def one(k, _):
             peer = (me + k) % replicas
@@ -132,9 +157,6 @@
         def _():
             pl.semaphore_wait(barrier, 3 * replicas - 1)
 
-        to_plane(sec, lambda _: tmsg.at[m], tbuf.at[m, me], t_send, t_recv.at[m], 1)
-        tbuf[m, me] = tmsg[m]
-
         @pl.when(sec < last)
         def _():
             for src, dst, send, recv in ((cmsg, crecv, c_send, c_recv), (nsend, nrecv, n_send, n_recv)):
@@ -142,6 +164,9 @@
                     src_ref=src.at[m], dst_ref=dst.at[m], send_sem=send, recv_sem=recv.at[m],
                     device_id={"section": above, "dp": me}, device_id_type=MESH,
                 ).start()
+
+        to_plane(sec, lambda _: tmsg.at[m], tbuf.at[m, me], t_send, t_recv.at[m], 1)
+        tbuf[m, me] = tmsg[m]
 
         @pl.when(sec == last)
         def _():
@@ -169,12 +194,14 @@
 
         @pl.when(sec > 0)
         def _():
+            for c in range(chunks):
+                x = x_v[m, :, :, lanes(c)].astype(f32).reshape(rows, LANES)
+                ones[:, lanes(c)] = convolve(jnp.where(x > 0, 1.0, 0.0), c)
             wait_bytes(nrecv.at[m], n_recv.at[m])
             wait_bytes(crecv.at[m], c_recv.at[m])
             for c in range(chunks):
                 x = x_v[m, :, :, lanes(c)].astype(f32).reshape(rows, LANES)
                 low = nrecv[m, :, lanes(c)].astype(f32)
-                ones[:, lanes(c)] = convolve(jnp.where(x > 0, 1.0, 0.0), c)
                 lows[:, lanes(c)] = convolve(jnp.where(x > 0, low, 0.0), c)
 
     def critical(m):
@@ -193,12 +220,17 @@
         def _():
             wait_bytes(obuf.at[m, pl.ds(0, replicas - 1)], o_recv.at[m])
             sbuf[m] = jnp.sum(obuf[m], axis=0)
+            dbuf[m] = jnp.zeros(dbuf.shape[1:], bf16)
 
         @pl.when(sec < last)
         def _():
+            if far:
+                wait_bytes(dbuf.at[m], d_recv.at[m])
             wait_bytes(sbuf.at[m], s_recv.at[m])
 
         total = sbuf[m]
+        if far:
+            total = total + jnp.sum(dbuf[m].astype(f32), axis=0)
         center, inv_std = stat[0:chunks, :], stat[chunks:, :]
         sum_grad = total[:chunks]
         cross = inv_std * (total[chunks:] - center * sum_grad)
@@ -220,8 +252,12 @@
                 mixed = base[chunks + c : chunks + c + 1, :] + row_sum(grad * lows[:, lanes(c)])
                 smsg[m, c : c + 1, :] = plain
                 smsg[m, chunks + c : chunks + c + 1, :] = mixed + crecv[m, c : c + 1, :] * plain
-            to_plane(sec, lambda _: smsg.at[m], pbuf.at[m, me], p_send, p_recv.at[m], 1)
-            pbuf[m, me] = smsg[m]
+            if far:
+                dmsg[m] = smsg[m].astype(bf16)
+            for k, o in enumerate(far):
+                to_peer(dmsg.at[m], dbuf.at[m, k], d_send, d_recv.at[m], below, device_at(o))
+            for k, o in enumerate(near):
+                to_peer(smsg.at[m], pbuf.at[m, k], p_send, p_recv.at[m], sec, device_at(o))
 
         for c in range(chunks):
             parts = columns_of(dgs[:, lanes(c)], width)[::-1]
@@ -246,12 +282,9 @@
     def hand_down(m):
         @pl.when(sec > 0)
         def _():
-            wait_bytes(pbuf.at[m, pl.ds(0, replicas - 1)], p_recv.at[m])
-            fmsg[m] = jnp.sum(pbuf[m], axis=0)
-            pltpu.make_async_remote_copy(
-                src_ref=fmsg.at[m], dst_ref=sbuf.at[m], send_sem=f_send, recv_sem=s_recv.at[m],
-                device_id={"section": below, "dp": me}, device_id_type=MESH,
-            ).start()
+            wait_bytes(pbuf.at[m], p_recv.at[m])
+            fmsg[m] = smsg[m] + jnp.sum(pbuf[m], axis=0)
+            to_peer(fmsg.at[m], sbuf.at[m], f_send, s_recv.at[m], below, me)
 
     def weights(m):
         pacc[...] += lax.dot_general(
@@ -269,38 +302,63 @@
                     kacc[r // per, r % per : r % per + 1, :] += row_sum(active * moved)
 
     def backward(m, _):
-        prepare(m)
         critical(m)
         weights(m)
+
+        @pl.when(m < micros - 1)
+        def _():
+            prepare(m + 1)
+
         hand_down(m)
         return 0
 
+    prepare(0)
     lax.fori_loop(0, micros, backward, 0)
 
-    for c in range(chunks):
-        bgrad[0:1, lanes(c)] = gacc[c : c + 1, :]
-        ggrad[0:1, lanes(c)] = gacc[chunks + c : chunks + c + 1, :]
-
-    rs_src[...] = pacc[...].reshape(rs_src.shape).astype(bf16)
-    to_plane(sec, lambda peer: rs_src.at[peer], rs_buf.at[me], rs_send, rs_recv, 1)
+    per = kacc.shape[1]
+    for k in range(2 * chunks):
+        r = 9 * chunks + k
+        kacc[r // per, r % per : r % per + 1, :] = jnp.where(me == 0, gacc[k : k + 1, :], 0.0)
+
+    half = channels // 2
+    chip, mate = me // 2, me + 1 - 2 * core
+    chips = replicas // 2
+    others = [o for o in offsets(ys, xs, 0)[0] if o[2] == 0]
+    mine, its = pl.ds(pl.multiple_of(core * half, half), half), pl.ds(pl.multiple_of((1 - core) * half, half), half)
+    pair_src[...] = pacc[its, :].astype(bf16)
+    to_peer(pair_src, pair_buf, w_send, w_recv, sec, mate)
     to_plane(sec, lambda peer: kacc.at[peer], krs_buf.at[me], ks_send, ks_recv, 1)
-    rs_buf[me] = rs_src[me]
     krs_buf[me] = kacc[me]
-    wait_bytes(rs_buf.at[pl.ds(0, replicas - 1)], rs_recv)
-    ag_src[...] = jnp.sum(rs_buf[...].astype(f32), axis=0).astype(bf16)
-    to_plane(sec, lambda _: ag_src, ag_buf.at[me], ag_send, ag_recv, 1)
+    wait_bytes(pair_buf, w_recv)
+    rs_src[...] = (pacc[mine, :] + pair_buf[...].astype(f32)).astype(bf16).reshape(rs_src.shape)
+    for o in others:
+        peer = device_at(o)
+        to_peer(rs_src.at[peer // 2], rs_buf.at[chip], rs_send, rs_recv, sec, peer)
+    rs_buf[chip] = rs_src[chip]
     wait_bytes(krs_buf.at[pl.ds(0, replicas - 1)], ks_recv)
     kag_src[...] = jnp.sum(krs_buf[...], axis=0)
+    wait_bytes(rs_buf.at[pl.ds(0, chips - 1)], rs_recv)
+    ag_src[...] = jnp.sum(rs_buf[...].astype(f32), axis=0).astype(bf16)
+    for k, o in enumerate(others):
+        to_peer(ag_src, ag_buf.at[core, chip], ag_send, ag_recv.at[k], sec, device_at(o))
+    to_peer(ag_src, ag_buf.at[core, chip], ag_send, m_recv, sec, mate)
+    ag_buf[core, chip] = ag_src[...]
     to_plane(sec, lambda _: kag_src, kag_buf.at[me], kg_send, kg_recv, 1)
-    ag_buf[me] = ag_src[...]
     kag_buf[me] = kag_src[...]
+    for k, o in reversed(list(enumerate(others))):
+        source = device_at((-o[0], -o[1], 0)) // 2
+        wait_bytes(ag_src, ag_recv.at[k])
+        to_peer(ag_buf.at[core, source], ag_buf.at[core, source], m_send, m_recv, sec, mate)
     wait_bytes(kag_buf.at[pl.ds(0, replicas - 1)], kg_recv)
-    per = kacc.shape[1]
     for t in range(9):
         for c in range(chunks):
             r = t * chunks + c
             kgrad[0, t // 3, t % 3 : t % 3 + 1, lanes(c)] = kag_buf[r // per, r % per : r % per + 1, :]
-    wait_bytes(ag_buf.at[pl.ds(0, replicas - 1)], ag_recv)
+    for c in range(chunks):
+        for at, ref in ((9, bgrad), (10, ggrad)):
+            r = at * chunks + c
+            ref[0:1, lanes(c)] = kag_buf[r // per, r % per : r % per + 1, :]
+    wait_bytes(ag_buf.at[0], m_recv)
     point[0] = ag_buf[...].reshape(channels, channels)
 
     for m in range(micros):
@@ -319,24 +377,65 @@
     @pl.when(sec > 0)
     def _():
         wait_bytes(usend, u_send)
-        wait_bytes(pbuf.at[:, pl.ds(0, replicas - 1)], p_send)
+        wait_bytes(pbuf, p_send)
+        if far:
+            wait_bytes(dbuf, d_send)
         wait_bytes(fmsg, f_send)
 
-    wait_bytes(rs_buf.at[pl.ds(0, replicas - 1)], rs_send)
+    wait_bytes(pair_src, w_send)
+    wait_bytes(rs_buf.at[pl.ds(0, chips - 1)], rs_send)
+    wait_bytes(rs_buf.at[pl.ds(0, chips - 1)], m_send)
     wait_bytes(krs_buf.at[pl.ds(0, replicas - 1)], ks_send)
-    wait_bytes(ag_buf.at[pl.ds(0, replicas - 1)], ag_send)
+    wait_bytes(rs_buf, ag_send)
     wait_bytes(kag_buf.at[pl.ds(0, replicas - 1)], kg_send)
+
+
+def finish(grads, point, kgrad, ggrad, bgrad, grads_out, point_out, kgrad_out, ggrad_out, bgrad_out, held, narrow, wide, in_sem, out_sem, p_in, p_out):
+    parts = grads.shape[1]
+    share = point.shape[1] // parts
+
+    def copies(m):
+        at = pl.ds(m * share, share)
+        return (
+            pltpu.make_async_copy(point.at[0, at], narrow.at[at], p_in.at[m]),
+            pltpu.make_async_copy(grads.at[0, m], held.at[m], in_sem.at[m]),
+            pltpu.make_async_copy(wide.at[at], point_out.at[0, at], p_out.at[m]),
+            pltpu.make_async_copy(held.at[m], grads_out.at[0, m], out_sem.at[m]),
+        )
+
+    for m in range(parts):
+        copies(m)[0].start()
+        copies(m)[1].start()
+    for t in range(9):
+        kgrad_out[t // 3, t % 3, 0:1, :] = kgrad[0, t // 3, t % 3 : t % 3 + 1, :]
+    ggrad_out[...] = ggrad[...]
+    bgrad_out[...] = bgrad[...]
+    for m in range(parts):
+        at = slice(m * share, (m + 1) * share)
+        point_in, grads_in, point_back, grads_back = copies(m)
+        point_in.wait()
+        wide[at, :] = narrow[at, :].astype(jnp.float32)
+        point_back.start()
+        grads_in.wait()
+        grads_back.start()
+    for m in range(parts):
+        copies(m)[2].wait()
+        copies(m)[3].wait()
 
 
 def solution(mesh):
     sections, replicas = mesh.shape["section"], mesh.shape["dp"]
+    chips = replicas // 2
+    ys = max(y for y in range(1, chips + 1) if y * y <= chips and chips % y == 0)
+    xs = chips // ys
+    far, near = offsets(ys, xs, REACH)
 
     def body(acts, out_grad, depth_kernel, point_weight, bn_gain):
         micros, _, height, width, channels = acts.shape[1:]
         rows = height * width
         chunks = channels // LANES
         share = channels // replicas
-        per = -(-9 * chunks // replicas)
+        per = -(-11 * chunks // replicas)
         f32, bf16 = jnp.float32, jnp.bfloat16
         image = (micros, height, width, channels)
         flat = (micros, rows, channels)
@@ -344,8 +443,8 @@
         vmem, dma = pltpu.VMEM, pltpu.SemaphoreType.DMA
         any_space = pl.BlockSpec(memory_space=pl.ANY)
         in_vmem = pl.BlockSpec(memory_space=pltpu.VMEM)
-        grads, point, kgrad, ggrad, bgrad = pl.pallas_call(
-            functools.partial(kernel, sections, replicas, micros, height, width, channels),
+        results = pl.pallas_call(
+            functools.partial(kernel, ys, xs, far, near, sections, replicas, micros, height, width, channels),
             out_shape=(
                 jax.ShapeDtypeStruct(acts.shape, bf16),
                 jax.ShapeDtypeStruct((1, channels, channels), bf16),
@@ -361,23 +460,42 @@
                 vmem(image, bf16), vmem(image, bf16), vmem((rows, channels), bf16), vmem((rows, channels), f32),
                 vmem((rows, channels), f32), vmem((rows, channels), f32), vmem(sums, f32),
                 vmem((micros, chunks, LANES), f32), vmem((micros, chunks, LANES), f32),
+                vmem((micros, *sums), bf16), vmem((micros, max(len(far), 1), *sums), bf16),
                 vmem((micros, *sums), f32), vmem((micros, *sums), f32),
-                vmem((micros, replicas, *sums), f32), vmem((micros, *sums), f32),
+                vmem((micros, len(near), *sums), f32), vmem((micros, *sums), f32),
                 vmem((micros, replicas, *sums), f32), vmem((micros, *sums), f32),
                 vmem((micros, replicas, *sums), f32), vmem((micros, *sums), f32),
                 vmem(sums, f32), vmem(sums, f32),
                 vmem((channels, channels), f32),
-                vmem((replicas, share, channels), bf16), vmem((replicas, share, channels), bf16),
-                vmem((share, channels), bf16), vmem((replicas, share, channels), bf16),
+                vmem((channels // 2, channels), bf16), vmem((channels // 2, channels), bf16),
+                vmem((chips, share, channels), bf16), vmem((chips, share, channels), bf16),
+                vmem((share, channels), bf16), vmem((2, chips, share, channels), bf16),
                 vmem((replicas, per, LANES), f32), vmem((replicas, per, LANES), f32),
                 vmem((per, LANES), f32), vmem((replicas, per, LANES), f32),
                 dma((micros + 1,)), dma((micros,)), dma((micros,)),
                 *[dma, dma((micros,))] * 7,
-                dma, dma, dma, dma, dma, dma, dma, dma,
+                dma, dma((micros,)), dma, dma, dma, dma, dma, dma((chips - 1,)), dma, dma, dma, dma, dma, dma,
             ],
             compiler_params=pltpu.CompilerParams(collective_id=0, has_side_effects=True),
         )(acts, out_grad, depth_kernel, point_weight, bn_gain)
-        return grads, point.astype(f32), kgrad, ggrad, bgrad
+        grads, point, kgrad, ggrad, bgrad = pl.pallas_call(
+            finish,
+            out_shape=(
+                jax.ShapeDtypeStruct(acts.shape, bf16),
+                jax.ShapeDtypeStruct((1, channels, channels), f32),
+                jax.ShapeDtypeStruct((3, 3, 1, channels), f32),
+                jax.ShapeDtypeStruct((1, channels), f32),
+                jax.ShapeDtypeStruct((1, channels), f32),
+            ),
+            in_specs=[any_space, any_space, in_vmem, in_vmem, in_vmem],
+            out_specs=(any_space, any_space, in_vmem, in_vmem, in_vmem),
+            scratch_shapes=[
+                vmem((micros, *acts.shape[2:]), bf16),
+                vmem((channels, channels), bf16), vmem((channels, channels), f32),
+                *[dma((micros,))] * 4,
+            ],
+        )(*results)
+        return grads, point, jnp.transpose(kgrad, (2, 0, 1, 3)), ggrad, bgrad
 
     return jax.shard_map(
         body,

time: 196 us -> 177 us (0.903)
  Pallas kernels: 189 us -> 176 us
  local copies, waits for them, and re-layouts: 3.5 us -> 0 us
  other arithmetic: 2.22 us -> 0 us
    pallas_call x1 -> x2, Pallas kernels: 189 us -> 176 us  [the longest x1 172 us: body(): pl.pallas_call(functools.partial(kernel, ys, xs, far, near, sections, rep...]
    unnamed x10 -> x0, local copies, waits for them, and re-layouts: 3.5 us -> none
    convert_element_type x1 -> x0, other arithmetic: 2.22 us -> none  [body(): return (grads, point.astype(f32), kgrad, ggrad, bgrad)]
where the time goes in v3:
time: 177 us; the launch traced here: 176 us
  Pallas kernels  176 us (99%)
    pallas_call x1, Pallas kernels, body(): pl.pallas_call(functools.partial(kernel, ys, xs, far, near, sections, rep...  172 us
    pallas_call x1, Pallas kernels, body(): pl.pallas_call(finish, out_shape=(jax.ShapeDtypeStruct(acts.shape, bf16),...  3.65 us

profile of v3, /device:TPU:1, one launch (start us, length us, event | category | flops | bytes accessed | tf_op | source)
XLA Modules:
  0.0 176.5 jit_solution(15092081125504361659)
XLA Ops:
  0.6 172.2 %shard_map.92 = (bf16[1,4,1,12,16,512]{5,4,3,2,1,0:T(8,128)(2,1)}, bf16[1,512,512]{2,1,0:T(8,128)(2,1)}, f32[1,3,3,512]{3,2,1,0:T(4,128)}, f32[1,512]{1,0:T(1,128)}, f32[1,512]{1,0:T(1,128)}) custom-call(bf16[1,4,1,12,16,512]{5,4,3,2,1,0:T(8,128)(2,1)} %acts.1, bf16[4,1,12,16,512]{4,3,2,1,0:T(8,128)(2,1)} %out_grad.1, bf16[1,3,3,512]{3,2,1,0:T(4,128)(2,1)} %kern.1, ...), custom_call_target="tpu_custom_call" | custom-call | tf_op jit(solution)/shard_map/pallas_call | solution.py:446
  172.8 3.7 %shard_map.93 = (bf16[1,4,1,12,16,512]{5,4,3,2,1,0:T(8,128)(2,1)}, f32[1,512,512]{2,1,0:T(8,128)}, f32[3,3,1,512]{3,2,1,0:T(1,128)}, f32[1,512]{1,0:T(1,128)}, f32[1,512]{1,0:T(1,128)}) custom-call(bf16[1,4,1,12,16,512]{5,4,3,2,1,0:T(8,128)(2,1)} %get-tuple-element.15.grads, bf16[1,512,512]{2,1,0:T(8,128)(2,1)} %get-tuple-element.16.point, ...), custom_call_target="tpu_custom_call" | custom-call | tf_op jit(solution)/shard_map/pallas_call | solution.py:481

commit v4 on v3

--- a/solution.py
+++ b/solution.py
@@ -10,7 +10,7 @@
 MESH = pl.DeviceIdType.MESH
 epsilon = 1e-05
 LANES = 128
-REACH = 2
+BEFORE, FIRST = 1, 1
 
 
 def columns_of(x, width):
@@ -33,25 +33,23 @@
     return min(a, n - a)
 
 
-def offsets(ys, xs, reach):
-    every = [(y, x, c) for y in range(ys) for x in range(xs) for c in range(2) if (y, x, c) != (0, 0, 0)]
-    every.sort(key=lambda o: -(ring(o[0], ys) + ring(o[1], xs)))
-    far = [o for o in every if ring(o[0], ys) + ring(o[1], xs) > reach]
-    return far, [o for o in every if o not in far]
+def offsets(ys, xs):
+    every = [(y, x, 0) for y in range(ys) for x in range(xs)]
+    return sorted(every, key=lambda o: -(ring(o[0], ys) + ring(o[1], xs)))
 
 
 def kernel(
-    ys, xs, far, near,
+    ys, xs,
     sections, replicas, micros, height, width, channels,
     acts, out_grad, kern, weight, gain,
     out, point, kgrad, ggrad, bgrad,
     x_v, w_v, kf, depth, normed, nsend, nrecv, ubuf, usend, pgs, dgs,
     ones, lows, base, cmsg, crecv,
-    dmsg, dbuf, sbuf, fmsg, pbuf, smsg, obuf, omsg, tbuf, tmsg, stat, gacc,
+    mbuf, dmsg, dbuf, hmsg, hbuf, sums_of, smsg, obuf, omsg, tbuf, tmsg, stat, gacc,
     pacc, pair_src, pair_buf, rs_src, rs_buf, ag_src, ag_buf, kacc, krs_buf, kag_src, kag_buf,
     in_sem, og_sem, out_sem,
-    t_send, t_recv, n_send, n_recv, c_send, c_recv, u_send, u_recv, p_send, p_recv, f_send, s_recv, o_send, o_recv,
-    d_send, d_recv, w_send, w_recv, rs_send, rs_recv, ag_send, ag_recv, m_send, m_recv, ks_send, ks_recv, kg_send, kg_recv,
+    t_send, t_recv, n_send, n_recv, c_send, c_recv, u_send, u_recv, x_send, x_recv, d_send, d_recv, o_send, o_recv,
+    h_send, h_recv, w_send, w_recv, rs_send, rs_recv, ag_send, ag_recv, m_send, m_recv, ks_send, ks_recv, kg_send, kg_recv,
 ):
     f32, bf16 = jnp.float32, jnp.bfloat16
     sec = lax.axis_index("section")
@@ -107,6 +105,8 @@
         return down(line[0], width) + line[1] + up(line[2], width)
 
     core, at_x, at_y = me % 2, (me // 2) % xs, me // (2 * xs)
+    mate = me + 1 - 2 * core
+    chips_from = offsets(ys, xs)
 
     def device_at(offset):
         dy, dx, dc = offset
@@ -205,61 +205,51 @@
                 lows[:, lanes(c)] = convolve(jnp.where(x > 0, low, 0.0), c)
 
     def critical(m):
+        @pl.when(sec == last)
+        def _():
+            wait_bytes(obuf.at[m, pl.ds(0, replicas - 1)], o_recv.at[m])
+            sums_of[...] = jnp.sum(obuf[m], axis=0).reshape(sums_of.shape)
+
         @pl.when(sec < last)
         def _():
-            wait_bytes(ubuf.at[m], u_recv.at[m])
-
-        @pl.when(sec > 0)
-        def _():
-            for c in range(chunks):
+            wait_bytes(dbuf.at[m], d_recv.at[m])
+            hmsg[m] = jnp.sum(dbuf[m].astype(f32), axis=0)
+            to_peer(hmsg.at[m], hbuf.at[m], h_send, h_recv.at[m], sec, mate)
+            sums_of[core] = hmsg[m]
+            wait_bytes(hbuf.at[m], h_recv.at[m])
+            sums_of[1 - core] = hbuf[m]
+
+        center, inv_std = stat[0:chunks, :], stat[chunks:, :]
+        sum_grad = sums_of[0]
+        cross = inv_std * (sums_of[1] - center * sum_grad)
+        gacc[0:chunks, :] += sum_grad
+        gacc[chunks:, :] += cross
+        half = channels // 2
+        for h in range(2):
+
+            @pl.when(sec < last)
+            def _():
+                wait_bytes(ubuf.at[m, :, :, pl.ds(h * half, half)], u_recv.at[m, h])
+
+            for c in range(h * chunks // 2, (h + 1) * chunks // 2):
+                scale = gain[0:1, lanes(c)] * inv_std[c : c + 1]
+                shift = scale * sum_grad[c : c + 1] / count
+                slope = scale * cross[c : c + 1] / count
                 u = ubuf[m, :, :, lanes(c)].astype(f32).reshape(rows, LANES)
+                pgs[:, lanes(c)] = (scale * u - shift - slope * normed[m, :, lanes(c)]).astype(bf16)
                 base[c : c + 1, :] = row_sum(u)
                 base[chunks + c : chunks + c + 1, :] = row_sum(u * nrecv[m, :, lanes(c)].astype(f32))
-
-        @pl.when(sec == last)
-        def _():
-            wait_bytes(obuf.at[m, pl.ds(0, replicas - 1)], o_recv.at[m])
-            sbuf[m] = jnp.sum(obuf[m], axis=0)
-            dbuf[m] = jnp.zeros(dbuf.shape[1:], bf16)
-
-        @pl.when(sec < last)
-        def _():
-            if far:
-                wait_bytes(dbuf.at[m], d_recv.at[m])
-            wait_bytes(sbuf.at[m], s_recv.at[m])
-
-        total = sbuf[m]
-        if far:
-            total = total + jnp.sum(dbuf[m].astype(f32), axis=0)
-        center, inv_std = stat[0:chunks, :], stat[chunks:, :]
-        sum_grad = total[:chunks]
-        cross = inv_std * (total[chunks:] - center * sum_grad)
-        gacc[0:chunks, :] += sum_grad
-        gacc[chunks:, :] += cross
-        for c in range(chunks):
-            scale = gain[0:1, lanes(c)] * inv_std[c : c + 1]
-            shift = scale * sum_grad[c : c + 1] / count
-            slope = scale * cross[c : c + 1] / count
-            u = ubuf[m, :, :, lanes(c)].astype(f32).reshape(rows, LANES)
-            pgs[:, lanes(c)] = (scale * u - shift - slope * normed[m, :, lanes(c)]).astype(bf16)
-        dgs[...] = lax.dot_general(pgs[...], w_v[...], (((1,), (1,)), ((), ())), preferred_element_type=f32)
-
-        @pl.when(sec > 0)
-        def _():
-            for c in range(chunks):
-                grad = dgs[:, lanes(c)]
-                plain = base[c : c + 1, :] + row_sum(grad * ones[:, lanes(c)])
-                mixed = base[chunks + c : chunks + c + 1, :] + row_sum(grad * lows[:, lanes(c)])
-                smsg[m, c : c + 1, :] = plain
-                smsg[m, chunks + c : chunks + c + 1, :] = mixed + crecv[m, c : c + 1, :] * plain
-            if far:
-                dmsg[m] = smsg[m].astype(bf16)
-            for k, o in enumerate(far):
-                to_peer(dmsg.at[m], dbuf.at[m, k], d_send, d_recv.at[m], below, device_at(o))
-            for k, o in enumerate(near):
-                to_peer(smsg.at[m], pbuf.at[m, k], p_send, p_recv.at[m], sec, device_at(o))
-
-        for c in range(chunks):
+            at = slice(h * half, (h + 1) * half)
+            term = lax.dot_general(pgs[:, at], w_v[:, at], (((1,), (1,)), ((), ())), preferred_element_type=f32)
+            dgs[...] = term if h == 0 else dgs[...] + term
+
+        def send_on(c):
+            to_peer(
+                usend.at[m, :, :, pl.ds(c * LANES, LANES)], ubuf.at[m, :, :, pl.ds(c * LANES, LANES)],
+                u_send, u_recv.at[m, c * 2 // chunks], below, me,
+            )
+
+        def gradient(c):
             parts = columns_of(dgs[:, lanes(c)], width)[::-1]
             line = [sum(tap(i, j, c) * parts[j] for j in range(3)) for i in range(3)]
             back = up(line[0], width) + line[1] + down(line[2], width)
@@ -268,23 +258,39 @@
             result = (u + jnp.where(x > 0, back, 0.0)).astype(bf16)
             usend[m, :, :, lanes(c)] = result.reshape(height, width, LANES)
 
-            @pl.when(sec > 0)
-            def _():
-                pltpu.make_async_remote_copy(
-                    src_ref=usend.at[m, :, :, pl.ds(c * LANES, LANES)],
-                    dst_ref=ubuf.at[m, :, :, pl.ds(c * LANES, LANES)],
-                    send_sem=u_send, recv_sem=u_recv.at[m],
-                    device_id={"section": below, "dp": me}, device_id_type=MESH,
-                ).start()
+        for c in range(BEFORE):
+            gradient(c)
+
+        @pl.when(sec > 0)
+        def _():
+            for c in range(BEFORE):
+                send_on(c)
+            for c in range(chunks):
+                grad = dgs[:, lanes(c)]
+                plain = base[c : c + 1, :] + row_sum(grad * ones[:, lanes(c)])
+                mixed = base[chunks + c : chunks + c + 1, :] + row_sum(grad * lows[:, lanes(c)])
+                smsg[m, 0, c : c + 1, :] = plain
+                smsg[m, 1, c : c + 1, :] = mixed + crecv[m, c : c + 1, :] * plain
+            to_peer(smsg.at[m, 1 - core], mbuf.at[m], x_send, x_recv.at[m], sec, mate)
+
+        for c in range(BEFORE, chunks):
+            gradient(c)
+            if c < FIRST:
+
+                @pl.when(sec > 0)
+                def _():
+                    send_on(c)
+
+        @pl.when(sec > 0)
+        def _():
+            wait_bytes(mbuf.at[m], x_recv.at[m])
+            dmsg[m] = (smsg[m, core] + mbuf[m]).astype(bf16)
+            for k, o in enumerate(chips_from):
+                to_peer(dmsg.at[m], dbuf.at[m, k], d_send, d_recv.at[m], below, device_at(o))
+            for c in range(FIRST, chunks):
+                send_on(c)
 
         pltpu.make_async_copy(usend.at[m], out.at[0, m, 0], out_sem.at[m]).start()
-
-    def hand_down(m):
-        @pl.when(sec > 0)
-        def _():
-            wait_bytes(pbuf.at[m], p_recv.at[m])
-            fmsg[m] = smsg[m] + jnp.sum(pbuf[m], axis=0)
-            to_peer(fmsg.at[m], sbuf.at[m], f_send, s_recv.at[m], below, me)
 
     def weights(m):
         pacc[...] += lax.dot_general(
@@ -308,9 +314,11 @@
         @pl.when(m < micros - 1)
         def _():
             prepare(m + 1)
-
-        hand_down(m)
         return 0
+
+    @pl.when(sec == 0)
+    def _():
+        nrecv[...] = jnp.zeros(nrecv.shape, bf16)
 
     prepare(0)
     lax.fori_loop(0, micros, backward, 0)
@@ -321,9 +329,9 @@
         kacc[r // per, r % per : r % per + 1, :] = jnp.where(me == 0, gacc[k : k + 1, :], 0.0)
 
     half = channels // 2
-    chip, mate = me // 2, me + 1 - 2 * core
+    chip = me // 2
     chips = replicas // 2
-    others = [o for o in offsets(ys, xs, 0)[0] if o[2] == 0]
+    others = chips_from[:-1]
     mine, its = pl.ds(pl.multiple_of(core * half, half), half), pl.ds(pl.multiple_of((1 - core) * half, half), half)
     pair_src[...] = pacc[its, :].astype(bf16)
     to_peer(pair_src, pair_buf, w_send, w_recv, sec, mate)
@@ -368,6 +376,7 @@
     @pl.when(sec < last)
     def _():
         wait_bytes(nsend, n_send)
+        wait_bytes(hbuf, h_send)
         wait_bytes(cmsg, c_send)
 
     @pl.when(sec == last)
@@ -377,10 +386,8 @@
     @pl.when(sec > 0)
     def _():
         wait_bytes(usend, u_send)
-        wait_bytes(pbuf, p_send)
-        if far:
-            wait_bytes(dbuf, d_send)
-        wait_bytes(fmsg, f_send)
+        wait_bytes(mbuf, x_send)
+        wait_bytes(dbuf, d_send)
 
     wait_bytes(pair_src, w_send)
     wait_bytes(rs_buf.at[pl.ds(0, chips - 1)], rs_send)
@@ -394,33 +401,34 @@
     parts = grads.shape[1]
     share = point.shape[1] // parts
 
-    def copies(m):
+    def point_copy(m, back):
         at = pl.ds(m * share, share)
-        return (
-            pltpu.make_async_copy(point.at[0, at], narrow.at[at], p_in.at[m]),
-            pltpu.make_async_copy(grads.at[0, m], held.at[m], in_sem.at[m]),
-            pltpu.make_async_copy(wide.at[at], point_out.at[0, at], p_out.at[m]),
-            pltpu.make_async_copy(held.at[m], grads_out.at[0, m], out_sem.at[m]),
-        )
+        if back:
+            return pltpu.make_async_copy(wide.at[at], point_out.at[0, at], p_out.at[m])
+        return pltpu.make_async_copy(point.at[0, at], narrow.at[at], p_in.at[m])
+
+    def grads_copy(m, back):
+        if back:
+            return pltpu.make_async_copy(held.at[m], grads_out.at[0, m], out_sem.at[m])
+        return pltpu.make_async_copy(grads.at[0, m], held.at[m], in_sem.at[m])
 
     for m in range(parts):
-        copies(m)[0].start()
-        copies(m)[1].start()
+        point_copy(m, False).start()
+        grads_copy(m, False).start()
     for t in range(9):
         kgrad_out[t // 3, t % 3, 0:1, :] = kgrad[0, t // 3, t % 3 : t % 3 + 1, :]
     ggrad_out[...] = ggrad[...]
     bgrad_out[...] = bgrad[...]
     for m in range(parts):
         at = slice(m * share, (m + 1) * share)
-        point_in, grads_in, point_back, grads_back = copies(m)
-        point_in.wait()
+        point_copy(m, False).wait()
         wide[at, :] = narrow[at, :].astype(jnp.float32)
-        point_back.start()
-        grads_in.wait()
-        grads_back.start()
+        point_copy(m, True).start()
+        grads_copy(m, False).wait()
+        grads_copy(m, True).start()
     for m in range(parts):
-        copies(m)[2].wait()
-        copies(m)[3].wait()
+        point_copy(m, True).wait()
+        grads_copy(m, True).wait()
 
 
 def solution(mesh):
@@ -428,7 +436,6 @@
     chips = replicas // 2
     ys = max(y for y in range(1, chips + 1) if y * y <= chips and chips % y == 0)
     xs = chips // ys
-    far, near = offsets(ys, xs, REACH)
 
     def body(acts, out_grad, depth_kernel, point_weight, bn_gain):
         micros, _, height, width, channels = acts.shape[1:]
@@ -439,12 +446,12 @@
         f32, bf16 = jnp.float32, jnp.bfloat16
         image = (micros, height, width, channels)
         flat = (micros, rows, channels)
-        sums = (2 * chunks, LANES)
+        sums, kind = (2 * chunks, LANES), (chunks, LANES)
         vmem, dma = pltpu.VMEM, pltpu.SemaphoreType.DMA
         any_space = pl.BlockSpec(memory_space=pl.ANY)
         in_vmem = pl.BlockSpec(memory_space=pltpu.VMEM)
         results = pl.pallas_call(
-            functools.partial(kernel, ys, xs, far, near, sections, replicas, micros, height, width, channels),
+            functools.partial(kernel, ys, xs, sections, replicas, micros, height, width, channels),
             out_shape=(
                 jax.ShapeDtypeStruct(acts.shape, bf16),
                 jax.ShapeDtypeStruct((1, channels, channels), bf16),
@@ -460,9 +467,8 @@
                 vmem(image, bf16), vmem(image, bf16), vmem((rows, channels), bf16), vmem((rows, channels), f32),
                 vmem((rows, channels), f32), vmem((rows, channels), f32), vmem(sums, f32),
                 vmem((micros, chunks, LANES), f32), vmem((micros, chunks, LANES), f32),
-                vmem((micros, *sums), bf16), vmem((micros, max(len(far), 1), *sums), bf16),
-                vmem((micros, *sums), f32), vmem((micros, *sums), f32),
-                vmem((micros, len(near), *sums), f32), vmem((micros, *sums), f32),
+                vmem((micros, *kind), f32), vmem((micros, *kind), bf16), vmem((micros, chips, *kind), bf16),
+                vmem((micros, *kind), f32), vmem((micros, *kind), f32), vmem((2, *kind), f32), vmem((micros, 2, *kind), f32),
                 vmem((micros, replicas, *sums), f32), vmem((micros, *sums), f32),
                 vmem((micros, replicas, *sums), f32), vmem((micros, *sums), f32),
                 vmem(sums, f32), vmem(sums, f32),
@@ -473,7 +479,7 @@
                 vmem((replicas, per, LANES), f32), vmem((replicas, per, LANES), f32),
                 vmem((per, LANES), f32), vmem((replicas, per, LANES), f32),
                 dma((micros + 1,)), dma((micros,)), dma((micros,)),
-                *[dma, dma((micros,))] * 7,
+                *[dma, dma((micros,))] * 3, dma, dma((micros, 2)), *[dma, dma((micros,))] * 3,
                 dma, dma((micros,)), dma, dma, dma, dma, dma, dma((chips - 1,)), dma, dma, dma, dma, dma, dma,
             ],
             compiler_params=pltpu.CompilerParams(collective_id=0, has_side_effects=True),

time: 177 us -> 171 us (0.966)
  Pallas kernels: 176 us -> 170 us
    pallas_call x1, Pallas kernels: 172 us -> 166 us  [body(): pl.pallas_call(functools.partial(kernel, ys, xs, sections, replicas, micr...]
where the time goes in v4:
time: 171 us; the launch traced here: 170 us
  Pallas kernels  170 us (99%)
    pallas_call x1, Pallas kernels, body(): pl.pallas_call(functools.partial(kernel, ys, xs, sections, replicas, micr...  166 us
    pallas_call x1, Pallas kernels, body(): pl.pallas_call(finish, out_shape=(jax.ShapeDtypeStruct(acts.shape, bf16),...  3.65 us

profile of v4, /device:TPU:1, one launch (start us, length us, event | category | flops | bytes accessed | tf_op | source)
XLA Modules:
  0.0 170.5 jit_solution(9371711142306633828)
XLA Ops:
  0.6 166.2 %shard_map.92 = (bf16[1,4,1,12,16,512]{5,4,3,2,1,0:T(8,128)(2,1)}, bf16[1,512,512]{2,1,0:T(8,128)(2,1)}, f32[1,3,3,512]{3,2,1,0:T(4,128)}, f32[1,512]{1,0:T(1,128)}, f32[1,512]{1,0:T(1,128)}) custom-call(bf16[1,4,1,12,16,512]{5,4,3,2,1,0:T(8,128)(2,1)} %acts.1, bf16[4,1,12,16,512]{4,3,2,1,0:T(8,128)(2,1)} %out_grad.1, bf16[1,3,3,512]{3,2,1,0:T(4,128)(2,1)} %kern.1, ...), custom_call_target="tpu_custom_call" | custom-call | tf_op jit(solution)/shard_map/pallas_call | solution.py:453
  166.8 3.7 %shard_map.93 = (bf16[1,4,1,12,16,512]{5,4,3,2,1,0:T(8,128)(2,1)}, f32[1,512,512]{2,1,0:T(8,128)}, f32[3,3,1,512]{3,2,1,0:T(1,128)}, f32[1,512]{1,0:T(1,128)}, f32[1,512]{1,0:T(1,128)}) custom-call(bf16[1,4,1,12,16,512]{5,4,3,2,1,0:T(8,128)(2,1)} %get-tuple-element.15.grads, bf16[1,512,512]{2,1,0:T(8,128)(2,1)} %get-tuple-element.16.point, ...), custom_call_target="tpu_custom_call" | custom-call | tf_op jit(solution)/shard_map/pallas_call | solution.py:487

commit v5 on v4

--- a/solution.py
+++ b/solution.py
@@ -41,9 +41,9 @@
 def kernel(
     ys, xs,
     sections, replicas, micros, height, width, channels,
-    acts, out_grad, kern, weight, gain,
+    acts, out_grad, kern_in, weight, gain_in,
     out, point, kgrad, ggrad, bgrad,
-    x_v, w_v, kf, depth, normed, nsend, nrecv, ubuf, usend, pgs, dgs,
+    kern, gain, x_v, w_v, kf, depth, normed, nsend, nrecv, ubuf, usend, pgs, dgs,
     ones, lows, base, cmsg, crecv,
     mbuf, dmsg, dbuf, hmsg, hbuf, sums_of, smsg, obuf, omsg, tbuf, tmsg, stat, gacc,
     pacc, pair_src, pair_buf, rs_src, rs_buf, ag_src, ag_buf, kacc, krs_buf, kag_src, kag_buf,
@@ -64,6 +64,9 @@
     def lanes(c):
         return slice(c * LANES, (c + 1) * LANES)
 
+    small = ((kern_in, kern, micros + 1), (gain_in, gain, micros + 2))
+    for src, dst, k in small:
+        pltpu.make_async_copy(src, dst, in_sem.at[k]).start()
     for m in range(micros):
         pltpu.make_async_copy(acts.at[0, m, 0], x_v.at[m], in_sem.at[m]).start()
         if m == 0:
@@ -89,6 +92,8 @@
 
     lax.fori_loop(0, replicas, greet, 0)
 
+    for src, dst, k in small:
+        pltpu.make_async_copy(src, dst, in_sem.at[k]).wait()
     for i in range(3):
         for j in range(3):
             kf[3 * i + j] = jnp.reshape(kern[0, i, j].astype(f32), (1, channels))
@@ -296,6 +301,8 @@
         pacc[...] += lax.dot_general(
             depth[m], pgs[...], (((0,), (0,)), ((), ())), preferred_element_type=f32
         )
+
+    def taps(m):
         per = kacc.shape[1]
         for c in range(chunks):
             x = x_v[m, :, :, lanes(c)].astype(f32).reshape(rows, LANES)
@@ -313,6 +320,7 @@
 
         @pl.when(m < micros - 1)
         def _():
+            taps(m)
             prepare(m + 1)
         return 0
 
@@ -322,11 +330,6 @@
 
     prepare(0)
     lax.fori_loop(0, micros, backward, 0)
-
-    per = kacc.shape[1]
-    for k in range(2 * chunks):
-        r = 9 * chunks + k
-        kacc[r // per, r % per : r % per + 1, :] = jnp.where(me == 0, gacc[k : k + 1, :], 0.0)
 
     half = channels // 2
     chip = me // 2
@@ -335,6 +338,13 @@
     mine, its = pl.ds(pl.multiple_of(core * half, half), half), pl.ds(pl.multiple_of((1 - core) * half, half), half)
     pair_src[...] = pacc[its, :].astype(bf16)
     to_peer(pair_src, pair_buf, w_send, w_recv, sec, mate)
+    taps(micros - 1)
+
+    per = kacc.shape[1]
+    for k in range(2 * chunks):
+        r = 9 * chunks + k
+        kacc[r // per, r % per : r % per + 1, :] = jnp.where(me == 0, gacc[k : k + 1, :], 0.0)
+
     to_plane(sec, lambda peer: kacc.at[peer], krs_buf.at[me], ks_send, ks_recv, 1)
     krs_buf[me] = kacc[me]
     wait_bytes(pair_buf, w_recv)
@@ -397,7 +407,10 @@
     wait_bytes(kag_buf.at[pl.ds(0, replicas - 1)], kg_send)
 
 
-def finish(grads, point, kgrad, ggrad, bgrad, grads_out, point_out, kgrad_out, ggrad_out, bgrad_out, held, narrow, wide, in_sem, out_sem, p_in, p_out):
+def finish(
+    grads, point, kgrad, ggrad, bgrad, grads_out, point_out, kgrad_out, ggrad_out, bgrad_out,
+    held, narrow, wide, k_in, k_out, g_held, b_held, in_sem, out_sem, p_in, p_out, s_in, s_out,
+):
     parts = grads.shape[1]
     share = point.shape[1] // parts
 
@@ -415,10 +428,10 @@
     for m in range(parts):
         point_copy(m, False).start()
         grads_copy(m, False).start()
-    for t in range(9):
-        kgrad_out[t // 3, t % 3, 0:1, :] = kgrad[0, t // 3, t % 3 : t % 3 + 1, :]
-    ggrad_out[...] = ggrad[...]
-    bgrad_out[...] = bgrad[...]
+    ins = [pltpu.make_async_copy(a, b, s_in.at[k]) for k, (a, b) in enumerate(((kgrad, k_in), (ggrad, g_held), (bgrad, b_held)))]
+    outs = [pltpu.make_async_copy(a, b, s_out.at[k]) for k, (a, b) in enumerate(((k_out, kgrad_out), (g_held, ggrad_out), (b_held, bgrad_out)))]
+    for copy in ins:
+        copy.start()
     for m in range(parts):
         at = slice(m * share, (m + 1) * share)
         point_copy(m, False).wait()
@@ -426,6 +439,14 @@
         point_copy(m, True).start()
         grads_copy(m, False).wait()
         grads_copy(m, True).start()
+    for copy in ins:
+        copy.wait()
+    for t in range(9):
+        k_out[t // 3, t % 3, 0:1, :] = k_in[0, t // 3, t % 3 : t % 3 + 1, :]
+    for copy in outs:
+        copy.start()
+    for copy in outs:
+        copy.wait()
     for m in range(parts):
         point_copy(m, True).wait()
         grads_copy(m, True).wait()
@@ -459,9 +480,10 @@
                 jax.ShapeDtypeStruct((1, channels), f32),
                 jax.ShapeDtypeStruct((1, channels), f32),
             ),
-            in_specs=[any_space, any_space, in_vmem, any_space, in_vmem],
+            in_specs=[any_space] * 5,
             out_specs=(any_space, in_vmem, in_vmem, in_vmem, in_vmem),
             scratch_shapes=[
+                vmem((1, 3, 3, channels), bf16), vmem((1, channels), f32),
                 vmem(image, bf16), vmem((channels, channels), bf16), vmem((9, 1, channels), f32),
                 vmem(flat, bf16), vmem(flat, f32), vmem(flat, bf16), vmem(flat, bf16),
                 vmem(image, bf16), vmem(image, bf16), vmem((rows, channels), bf16), vmem((rows, channels), f32),
@@ -478,7 +500,7 @@
                 vmem((share, channels), bf16), vmem((2, chips, share, channels), bf16),
                 vmem((replicas, per, LANES), f32), vmem((replicas, per, LANES), f32),
                 vmem((per, LANES), f32), vmem((replicas, per, LANES), f32),
-                dma((micros + 1,)), dma((micros,)), dma((micros,)),
+                dma((micros + 3,)), dma((micros,)), dma((micros,)),
                 *[dma, dma((micros,))] * 3, dma, dma((micros, 2)), *[dma, dma((micros,))] * 3,
                 dma, dma((micros,)), dma, dma, dma, dma, dma, dma((chips - 1,)), dma, dma, dma, dma, dma, dma,
             ],
@@ -493,12 +515,14 @@
                 jax.ShapeDtypeStruct((1, channels), f32),
                 jax.ShapeDtypeStruct((1, channels), f32),
             ),
-            in_specs=[any_space, any_space, in_vmem, in_vmem, in_vmem],
-            out_specs=(any_space, any_space, in_vmem, in_vmem, in_vmem),
+            in_specs=[any_space] * 5,
+            out_specs=(any_space,) * 5,
             scratch_shapes=[
                 vmem((micros, *acts.shape[2:]), bf16),
                 vmem((channels, channels), bf16), vmem((channels, channels), f32),
-                *[dma((micros,))] * 4,
+                vmem((1, 3, 3, channels), f32), vmem((3, 3, 1, channels), f32),
+                vmem((1, channels), f32), vmem((1, channels), f32),
+                *[dma((micros,))] * 4, dma((3,)), dma((3,)),
             ],
         )(*results)
         return grads, point, jnp.transpose(kgrad, (2, 0, 1, 3)), ggrad, bgrad

time: 171 us -> 168 us (0.982)
  Pallas kernels: 170 us -> 168 us
where the time goes in v5:
time: 168 us
  Pallas kernels  168 us (100%)
    pallas_call x1, Pallas kernels, body(): pl.pallas_call(functools.partial(kernel, ys, xs, sections, replicas, micr...  165 us

profile of v5, /device:TPU:1, one launch (start us, length us, event | category | flops | bytes accessed | tf_op | source)
XLA Modules:
  0.0 168.3 jit_solution(17783387080413315170)
XLA Ops:
  0.6 165.3 %shard_map.92 = (bf16[1,4,1,12,16,512]{5,4,3,2,1,0:T(8,128)(2,1)}, bf16[1,512,512]{2,1,0:T(8,128)(2,1)}, f32[1,3,3,512]{3,2,1,0:T(4,128)}, f32[1,512]{1,0:T(1,128)}, f32[1,512]{1,0:T(1,128)}) custom-call(bf16[1,4,1,12,16,512]{5,4,3,2,1,0:T(8,128)(2,1)} %acts.1, bf16[4,1,12,16,512]{4,3,2,1,0:T(8,128)(2,1)} %out_grad.1, bf16[1,3,3,512]{3,2,1,0:T(4,128)(2,1)} %kern_in.1, ...), custom_call_target="tpu_custom_call" | custom-call | tf_op jit(solution)/shard_map/pallas_call | solution.py:474
  165.9 2.4 %shard_map.93 = (bf16[1,4,1,12,16,512]{5,4,3,2,1,0:T(8,128)(2,1)}, f32[1,512,512]{2,1,0:T(8,128)}, f32[3,3,1,512]{3,2,1,0:T(1,128)}, f32[1,512]{1,0:T(1,128)}, f32[1,512]{1,0:T(1,128)}) custom-call(bf16[1,4,1,12,16,512]{5,4,3,2,1,0:T(8,128)(2,1)} %get-tuple-element.15.grads, bf16[1,512,512]{2,1,0:T(8,128)(2,1)} %get-tuple-element.16.point, ...), custom_call_target="tpu_custom_call" | custom-call | tf_op jit(solution)/shard_map/pallas_call | solution.py:509
